TPU v7x, 128 devices: a whole 4x4x4 slice. The times are simulated.
128 devices in a mesh: rep: 1, r: 16 (over y, z), s: 8 (over x, core).
Axes of the slice: x: 4, y: 4, z: 4, core: 2. Of those that a mesh axis runs over, the one named last changes fastest.
Arguments:
- x: bfloat16 [128, 2048, 1024], P(('rep', 'r', 's'))
- dy: bfloat16 [128, 2048, 1024], P(('rep', 'r', 's'))
- w_gate: bfloat16 [2, 1024, 3584], P(None, 's')
- w_up: bfloat16 [2, 1024, 3584], P(None, 's')
- w_down: bfloat16 [2, 3584, 1024], P(None, 's')
- m_w_gate: float32 [2, 1024, 3584], P(None, 's')
- m_w_up: float32 [2, 1024, 3584], P(None, 's')
- m_w_down: float32 [2, 3584, 1024], P(None, 's')
- v_w_gate: float32 [2, 1024, 3584], P(None, 's')
- v_w_up: float32 [2, 1024, 3584], P(None, 's')
- v_w_down: float32 [2, 3584, 1024], P(None, 's')
Outputs:
- output 1: bfloat16 [2, 1024, 3584], P('rep', 's')
- output 2: bfloat16 [2, 1024, 3584], P('rep', 's')
- output 3: bfloat16 [2, 3584, 1024], P('rep', 's')
- output 4: float32 [2, 1024, 3584], P('rep', 's')
- output 5: float32 [2, 1024, 3584], P('rep', 's')
- output 6: float32 [2, 3584, 1024], P('rep', 's')
- output 7: float32 [2, 1024, 3584], P('rep', 's')
- output 8: float32 [2, 1024, 3584], P('rep', 's')
- output 9: float32 [2, 3584, 1024], P('rep', 's')
All inputs are finite; a program needn't handle non-finite values.
Results may differ from a plain program's by a relative error of at most 0.022.
Values are sent between devices in bfloat16 or wider.
A program may use at most 1.5 GiB of HBM per device.

v0:
```python
import jax
import jax.numpy as jnp
from jax import lax
from jax.sharding import PartitionSpec as P

NAMES = ("w_gate", "w_up", "w_down")


def matmul(a, w):
    return jnp.dot(a, w, preferred_element_type=jnp.float32).astype(jnp.bfloat16)


def normed(h):
    wide = h.astype(jnp.float32)
    scale = lax.rsqrt(jnp.mean(wide**2, -1, keepdims=True) + 1e-6)
    return (wide * scale).astype(jnp.bfloat16)


def layer(h, w):
    a = normed(h)
    gate = jnp.dot(a, w["w_gate"], preferred_element_type=jnp.float32)
    up = jnp.dot(a, w["w_up"], preferred_element_type=jnp.float32)
    return h + matmul((jax.nn.silu(gate) * up).astype(jnp.bfloat16), w["w_down"])


def adamw(w, m, v, g):
    m = 0.9 * m + 0.1 * g
    v = 0.95 * v + 0.05 * g * g
    step = m * lax.rsqrt(v + 1e-8) + 0.1 * w
    return (w - 0.02 * step).astype(jnp.bfloat16), m, v


def solution(mesh):
    def fetched(weights, number):
        return {name: lax.all_gather(w[number], "s", axis=0, tiled=True) for name, w in zip(NAMES, weights, strict=True)}

    def summed(term):
        return lax.psum(lax.psum_scatter(term, "s", scatter_dimension=0, tiled=True), "r")

    def step(x, dy, *arrays):
        weights, m, v = (arrays[i : i + 3] for i in (0, 3, 6))
        layers = weights[0].shape[0]
        h, kept = x[0], []
        for number in range(layers):
            kept.append(h)
            h = layer(h, fetched(weights, number))
        by_h, mine = dy[0], [None] * layers
        for number in reversed(range(layers)):
            _, back = jax.vjp(lambda w, h: layer(h, w), fetched(weights, number), kept[number])
            by_w, by_h = back(by_h)
            mine[number] = [summed(by_w[name]) for name in NAMES]
        gradients = [jnp.stack([mine[number][i] for number in range(layers)]).astype(jnp.float32) for i in range(3)]
        new = [adamw(w.astype(jnp.float32), m, v, g) for w, m, v, g in zip(weights, m, v, gradients, strict=True)]
        return tuple(one[which] for which in range(3) for one in new)

    states, cut = P(("rep", "r", "s"), None, None), P(None, "s", None)
    return jax.shard_map(
        step,
        mesh=mesh,
        in_specs=(states, states) + (cut,) * 9,
        out_specs=(P("rep", "s", None),) * 9,
        check_vma=False,
    )
```

profile of v0, /device:TPU:0, one launch (start us, length us, event | category | flops | bytes accessed | tf_op | source)
XLA Modules:
  0.0 855.7 jit_solution(10076539350342264034)
XLA Ops:
  32.4 25.5 %all-gather.13.cloned.1.call-done = bf16[1,1024,3584]{2,1,0:T(8,128)(2,1)} async-done(((bf16[1,128,3584]{2,1,0:T(8,128)(2,1)}), bf16[1,1024,3584]{2,1,0:T(8,128)(2,1)}) %all-gather.13.cloned.1.call-update) | async-done | bytes 7340048 | tf_op jit(solution)/shard_map/all_gather | solution.py:35
  57.8 24.3 %fusion.41 = f32[2048,3584]{1,0:T(8,128)} fusion(bf16[1,1024,3584]{2,1,0:T(8,128)(2,1)} %all-gather.13.cloned.1.call-done, bf16[1,2048,1024]{1,2,0:T(8,128)(2,1)} %copy.20, f32[2048]{0:T(1024)S(1)} %add_rsqrt_fusion), kind=kOutput, calls=%fused_computation.59 | convolution fusion | flops 15038676992 | bytes 40902656 | tf_op jit(solution)/shard_map/dot_general | solution.py:21
  82.2 23.2 %all-gather.15.cloned.1.call-done = bf16[1,1024,3584]{2,1,0:T(8,128)(2,1)} async-done(((bf16[1,128,3584]{2,1,0:T(8,128)(2,1)}), bf16[1,1024,3584]{2,1,0:T(8,128)(2,1)}) %all-gather.15.cloned.1.call-update) | async-done | bytes 7340048 | tf_op jit(solution)/shard_map/all_gather | solution.py:35
  105.4 34.9 %multiply_convert_fusion.1 = (bf16[2048,3584]{1,0:T(8,128)(2,1)}, f32[2048,3584]{1,0:T(8,128)}) fusion(f32[2048,3584]{1,0:T(8,128)} %fusion.41, bf16[1,1024,3584]{2,1,0:T(8,128)(2,1)} %all-gather.15.cloned.1.call-done, bf16[1,2048,1024]{1,2,0:T(8,128)(2,1)} %copy.20, f32[2048]{0:T(1024)S(1)} %add_rsqrt_fusion), kind=kOutput, calls=%fused_computation.17 | convolution fusion | flops 15082717184 | bytes 84942848 | tf_op jit(solution)/shard_map/dot_general | solution.py:22
  152.9 21.9 %fusion.19 = (f32[2048]{0:T(1024)S(1)}, bf16[2048,1024]{0,1:T(8,128)(2,1)}) fusion(bf16[2048,3584]{1,0:T(8,128)(2,1)} %get-tuple-element.30, bf16[1,3584,1024]{2,1,0:T(8,128)(2,1)} %all-gather.17.cloned.1.call-done, bf16[1,2048,1024]{1,2,0:T(8,128)(2,1)} %copy.20), kind=kOutput, calls=%fused_computation.37 | convolution fusion | flops 15042869248 | bytes 30416896 | tf_op jit(solution)/shard_map/dot_general | solution.py:10
  175.4 24.9 %all-gather.21.cloned.1.call-done = bf16[1,3584,1024]{2,1,0:T(8,128)(2,1)} async-done(((bf16[1,448,1024]{2,1,0:T(8,128)(2,1)}), bf16[1,3584,1024]{2,1,0:T(8,128)(2,1)}) %all-gather.21.cloned.1.call-update) | async-done | bytes 7340048 | tf_op jit(solution)/shard_map/all_gather | solution.py:35
  200.3 22.2 %convolution_convert_fusion.1 = bf16[2048,3584]{1,0:T(8,128)(2,1)} fusion(bf16[1,3584,1024]{2,1,0:T(8,128)(2,1)} %all-gather.21.cloned.1.call-done, bf16[1,2048,1024]{2,1,0:T(8,128)(2,1)} %param.12), kind=kOutput, calls=%fused_computation.23 | convolution fusion | flops 15039725568 | bytes 26214400 | tf_op jit(solution)/shard_map/transpose(jvp())/dot_general | solution.py:10
  222.5 25.2 %all-gather.23.cloned.1.call-done = bf16[1,1024,3584]{2,1,0:T(8,128)(2,1)} async-done(((bf16[1,128,3584]{2,1,0:T(8,128)(2,1)}), bf16[1,1024,3584]{2,1,0:T(8,128)(2,1)}) %all-gather.23.cloned.1.call-update) | async-done | bytes 7340048 | tf_op jit(solution)/shard_map/all_gather | solution.py:35
  247.7 24.6 %fusion.28 = f32[2048,3584]{1,0:T(8,128)} fusion(bf16[1,1024,3584]{2,1,0:T(8,128)(2,1)} %all-gather.23.cloned.1.call-done, bf16[2048,1024]{0,1:T(8,128)(2,1)} %get-tuple-element.33, f32[2048]{0:T(1024)S(1)} %fusion.74), kind=kOutput, calls=%fused_computation.46 | convolution fusion | flops 15038676992 | bytes 40902656 | tf_op jit(solution)/shard_map/jvp()/dot_general | solution.py:22
  272.3 22.8 %all-gather.19.cloned.1.call-done = bf16[1,1024,3584]{2,1,0:T(8,128)(2,1)} async-done(((bf16[1,128,3584]{2,1,0:T(8,128)(2,1)}), bf16[1,1024,3584]{2,1,0:T(8,128)(2,1)}) %all-gather.19.cloned.1.call-update) | async-done | bytes 7340048 | tf_op jit(solution)/shard_map/all_gather | solution.py:35
  295.1 43.6 %fusion.2 = (bf16[2048,3584]{1,0:T(8,128)(2,1)}, f32[2048,3584]{1,0:T(8,128)}) fusion(f32[2048,3584]{1,0:T(8,128)} %fusion.28, bf16[2048,3584]{1,0:T(8,128)(2,1)} %convolution_convert_fusion.1, bf16[1,1024,3584]{2,1,0:T(8,128)(2,1)} %all-gather.19.cloned.1.call-done, bf16[2048,1024]{0,1:T(8,128)(2,1)} %get-tuple-element.33, f32[2048]{0:T(1024)S(1)} %fusion.74), kind=kOutput, calls=%fused_computation.8 | convolution fusion | flops 15126757376 | bytes 99622912 | tf_op jit(solution)/shard_map/jvp()/dot_general | solution.py:21
  338.6 24.3 %fusion.12 = bf16[2048,1024]{0,1:T(8,128)(2,1)} fusion(bf16[2048,3584]{1,0:T(8,128)(2,1)} %convolution_convert_fusion.1, bf16[1,1024,3584]{2,1,0:T(8,128)(2,1)} %all-gather.23.cloned.1.call-done, f32[2048,3584]{1,0:T(8,128)} %get-tuple-element.35), kind=kOutput, calls=%fused_computation.21 | convolution fusion | flops 15076425728 | bytes 55574528 | tf_op jit(solution)/shard_map/transpose(jvp())/dot_general | solution.py:22
  363.0 22.3 %fusion.21 = (f32[2048]{0:T(1024)S(1)}, bf16[2048,1024]{0,1:T(8,128)(2,1)}) fusion(bf16[2048,1024]{0,1:T(8,128)(2,1)S(1)} %copy-done.5, bf16[2048,1024]{0,1:T(8,128)(2,1)} %fusion.12, bf16[2048,3584]{1,0:T(8,128)(2,1)} %get-tuple-element.34, bf16[1,1024,3584]{2,1,0:T(8,128)(2,1)} %all-gather.19.cloned.1.call-done), kind=kOutput, calls=%fused_computation.39 | convolution fusion | flops 15042869248 | bytes 34611200 | tf_op jit(solution)/shard_map/transpose(jvp())/dot_general | solution.py:21
  392.2 20.7 %convolution_convert_fusion.2 = bf16[3584,1024]{1,0:T(8,128)(2,1)} fusion(bf16[2048,3584]{1,0:T(8,128)(2,1)} %get-tuple-element.30, bf16[2048,1024]{0,1:T(8,128)(2,1)S(1)} %fusion.44), kind=kOutput, calls=%fused_computation.44 | convolution fusion | flops 15036055552 | bytes 26214400 | tf_op jit(solution)/shard_map/transpose(jvp())/dot_general | solution.py:10
  412.9 27.5 %fusion.25 = bf16[3584,1024]{1,0:T(8,128)(2,1)} fusion(f32[2048,3584]{1,0:T(8,128)} %fusion.28, bf16[1,2048,1024]{2,1,0:T(8,128)(2,1)} %param.12, f32[2048,3584]{1,0:T(8,128)} %get-tuple-element.35), kind=kOutput, calls=%fused_computation.41 | convolution fusion | flops 15080095744 | bytes 70254592 | tf_op jit(solution)/shard_map/transpose(jvp())/dot_general | solution.py:10
  440.5 22.3 %convolution_convert_fusion = bf16[2048,3584]{1,0:T(8,128)(2,1)} fusion(bf16[2048,1024]{0,1:T(8,128)(2,1)} %copy-done.6, bf16[1,3584,1024]{2,1,0:T(8,128)(2,1)} %all-gather.17.cloned.1.call-done), kind=kOutput, calls=%fused_computation.22 | convolution fusion | flops 15039725568 | bytes 26214400 | tf_op jit(solution)/shard_map/transpose(jvp())/dot_general | solution.py:10
  462.8 26.2 %fusion.27 = bf16[1024,3584]{1,0:T(8,128)(2,1)} fusion(bf16[2048,3584]{1,0:T(8,128)(2,1)} %convolution_convert_fusion, f32[2048,3584]{1,0:T(8,128)} %fusion.41, bf16[1,2048,1024]{1,2,0:T(8,128)(2,1)} %copy.20, f32[2048]{0:T(1024)S(1)} %copy-done.16), kind=kOutput, calls=%fused_computation.43 | convolution fusion | flops 15086387200 | bytes 55582720 | tf_op jit(solution)/shard_map/transpose(jvp())/dot_general | solution.py:22
  489.7 25.9 %fusion.26 = bf16[1024,3584]{1,0:T(8,128)(2,1)} fusion(bf16[2048,3584]{1,0:T(8,128)(2,1)} %convolution_convert_fusion.1, bf16[2048,1024]{0,1:T(8,128)(2,1)} %get-tuple-element.33, f32[2048]{0:T(1024)S(1)} %copy-done.12, f32[2048,3584]{1,0:T(8,128)} %get-tuple-element.35), kind=kOutput, calls=%fused_computation.42 | convolution fusion | flops 15086387200 | bytes 55582720 | tf_op jit(solution)/shard_map/transpose(jvp())/dot_general | solution.py:22
  515.7 34.0 %fusion.22 = bf16[1024,3584]{1,0:T(8,128)(2,1)} fusion(f32[2048,3584]{1,0:T(8,128)} %fusion.41, f32[2048,3584]{1,0:T(8,128)} %get-tuple-element.31, bf16[2048,3584]{1,0:T(8,128)(2,1)} %convolution_convert_fusion, bf16[1,2048,1024]{1,2,0:T(8,128)(2,1)} %copy.20, f32[2048]{0:T(1024)S(1)} %copy-done.16), kind=kOutput, calls=%fused_computation.40 | convolution fusion | flops 15123087360 | bytes 84942848 | tf_op jit(solution)/shard_map/transpose(jvp())/dot_general | solution.py:21
  549.7 21.7 %convolution_convert_fusion.3 = bf16[1024,3584]{1,0:T(8,128)(2,1)} fusion(bf16[2048,3584]{1,0:T(8,128)(2,1)} %get-tuple-element.34, bf16[2048,1024]{0,1:T(8,128)(2,1)} %get-tuple-element.33, f32[2048]{0:T(1024)S(1)} %copy-done.12), kind=kOutput, calls=%fused_computation.45 | convolution fusion | flops 15038676992 | bytes 26222592 | tf_op jit(solution)/shard_map/transpose(jvp())/dot_general | solution.py:21
  571.6 37.8 %reduce-scatter.13.cloned.1.call-done = bf16[128,3584]{1,0:T(8,128)(2,1)} async-done(((bf16[1024,3584]{1,0:T(8,128)(2,1)}), bf16[128,3584]{1,0:T(8,128)(2,1)}) %reduce-scatter.13.cloned.1.call-update) | async-done | bytes 917520 | tf_op jit(solution)/shard_map/reduce_scatter | solution.py:38
  609.4 49.7 %reduce-scatter.7.cloned.1.call-done = bf16[128,3584]{1,0:T(8,128)(2,1)} async-done(((bf16[1024,3584]{1,0:T(8,128)(2,1)}), bf16[128,3584]{1,0:T(8,128)(2,1)}) %reduce-scatter.7.cloned.1.call-update) | async-done | bytes 917520 | tf_op jit(solution)/shard_map/reduce_scatter | solution.py:38
  659.1 49.5 %reduce-scatter.9.cloned.1.call-done = bf16[128,3584]{1,0:T(8,128)(2,1)} async-done(((bf16[1024,3584]{1,0:T(8,128)(2,1)}), bf16[128,3584]{1,0:T(8,128)(2,1)}) %reduce-scatter.9.cloned.1.call-update) | async-done | bytes 917520 | tf_op jit(solution)/shard_map/reduce_scatter | solution.py:38
  708.6 119.2 %all-reduce.3.cloned.1.call-done = (bf16[1,128,3584]{2,1,0:T(8,128)(2,1)}, bf16[1,128,3584]{2,1,0:T(8,128)(2,1)}, bf16[1,128,3584]{2,1,0:T(8,128)(2,1)}, bf16[1,...) async-done(((bf16[1,128,3584]{2,1,0:T(8,128)(2,1)}, bf16[1,128,3584]{2,1,0:T(8,128)(2,1)}, bf16[1,128,3584]{2,1,0:T(8,128)(2,1)}, ...) | async-done | bytes 5505040 | tf_op jit(solution)/shard_map/psum | solution.py:38
  (76 shorter events, 67.4 us)
Async XLA Ops:
  7.2 50.7 %all-gather.13.cloned.1.call-start = ((), (), s32[]{:S(2)}) async-start(), calls=%async_computation.12 | async-start | bytes 8257536 | tf_op jit(solution)/shard_map/all_gather | solution.py:35
  10.2 95.2 %all-gather.15.cloned.1.call-start = ((), (), s32[]{:S(2)}) async-start(), calls=%async_computation.13 | async-start | bytes 8257536 | tf_op jit(solution)/shard_map/all_gather | solution.py:35
  13.1 139.9 %all-gather.17.cloned.1.call-start = ((), (), s32[]{:S(2)}) async-start(), calls=%async_computation.14 | async-start | bytes 8257536 | tf_op jit(solution)/shard_map/all_gather | solution.py:35
  14.5 185.8 %all-gather.21.cloned.1.call-start = ((), (), s32[]{:S(2)}) async-start(), calls=%async_computation.16 | async-start | bytes 8257536 | tf_op jit(solution)/shard_map/all_gather | solution.py:35
  15.1 232.6 %all-gather.23.cloned.1.call-start = ((), (), s32[]{:S(2)}) async-start(), calls=%async_computation.17 | async-start | bytes 8257536 | tf_op jit(solution)/shard_map/all_gather | solution.py:35
  15.7 279.4 %all-gather.19.cloned.1.call-start = ((), (), s32[]{:S(2)}) async-start(), calls=%async_computation.15 | async-start | bytes 8257536 | tf_op jit(solution)/shard_map/all_gather | solution.py:35
  16.3 555.2 %reduce-scatter.15.cloned.1.call-start = ((), (), s32[]{:S(2)}) async-start(), calls=%async_computation.10 | async-start | bytes 8257536 | tf_op jit(solution)/shard_map/reduce_scatter | solution.py:38
  25.9 79.5 %copy-start.15 = (f32[2048]{0:T(1024)}, f32[2048]{0:T(1024)S(1)}, u32[]{:S(2)}) copy-start(f32[2048]{0:T(1024)S(1)} %add_rsqrt_fusion) | copy-start | bytes 24580
  175.4 209.9 %copy-start.11 = (f32[2048]{0:T(1024)}, f32[2048]{0:T(1024)S(1)}, u32[]{:S(2)}) copy-start(f32[2048]{0:T(1024)S(1)} %fusion.74) | copy-start | bytes 24580
  338.6 24.3 %copy-start.5 = (bf16[2048,1024]{0,1:T(8,128)(2,1)S(1)}, bf16[2048,1024]{0,1:T(8,128)(2,1)}, u32[]{:S(2)}) copy-start(bf16[2048,1024]{0,1:T(8,128)(2,1)} %get-tuple-element.33) | copy-start | bytes 12582916
  363.0 22.3 %copy-start.14 = (f32[2048]{0:T(1024)S(1)}, f32[2048]{0:T(1024)}, u32[]{:S(2)}) copy-start(f32[2048]{0:T(1024)} %copy-done.13) | copy-start | bytes 24580
  363.0 22.4 %copy-start = (bf16[1,2048,1024]{1,2,0:T(8,128)(2,1)S(1)}, bf16[1,2048,1024]{1,2,0:T(8,128)(2,1)}, u32[]{:S(2)}) copy-start(bf16[1,2048,1024]{1,2,0:T(8,128)(2,1)} %copy.21) | copy-start | bytes 12582916
  412.9 158.7 %reduce-scatter.17.cloned.1.call-start = ((), (), s32[]{:S(2)}) async-start(), calls=%async_computation.11 | async-start | bytes 8257536 | tf_op jit(solution)/shard_map/reduce_scatter | solution.py:38
  440.4 22.4 %copy-start.16 = (f32[2048]{0:T(1024)S(1)}, f32[2048]{0:T(1024)}, u32[]{:S(2)}) copy-start(f32[2048]{0:T(1024)} %copy-done.15) | copy-start | bytes 24580
  440.5 131.1 %reduce-scatter.11.cloned.1.call-start = ((), (), s32[]{:S(2)}) async-start(), calls=%async_computation.8 | async-start | bytes 8257536 | tf_op jit(solution)/shard_map/reduce_scatter | solution.py:38
  489.0 120.4 %reduce-scatter.13.cloned.1.call-start = ((), (), s32[]{:S(2)}) async-start(), calls=%async_computation.9 | async-start | bytes 8257536 | tf_op jit(solution)/shard_map/reduce_scatter | solution.py:38
  515.6 143.5 %reduce-scatter.7.cloned.1.call-start = ((), (), s32[]{:S(2)}) async-start(), calls=%async_computation.6 | async-start | bytes 8257536 | tf_op jit(solution)/shard_map/reduce_scatter | solution.py:38
  549.7 158.9 %reduce-scatter.9.cloned.1.call-start = ((), (), s32[]{:S(2)}) async-start(), calls=%async_computation.7 | async-start | bytes 8257536 | tf_op jit(solution)/shard_map/reduce_scatter | solution.py:38
  571.4 256.4 %copy-start.2 = (bf16[2,448,1024]{2,1,0:T(8,128)(2,1)S(1)}, bf16[2,448,1024]{2,1,0:T(8,128)(2,1)}, u32[]{:S(2)}) copy-start(bf16[2,448,1024]{2,1,0:T(8,128)(2,1)} %param.15) | copy-start | bytes 5505028
  571.4 256.4 %all-reduce.3.cloned.1.call-start = ((), (), s32[]{:S(2)}) async-start(), calls=%async_computation.18 | async-start | bytes 11010048 | tf_op jit(solution)/shard_map/psum | solution.py:38
  827.8 8.3 copy-start.7
  827.8 10.1 %copy-start.8 = (f32[2,128,3584]{2,1,0:T(8,128)S(1)}, f32[2,128,3584]{2,1,0:T(8,128)}, u32[]{:S(2)}) copy-start(f32[2,128,3584]{2,1,0:T(8,128)} %param.16) | copy-start | bytes 11010052
  827.8 10.2 %copy-start.9 = (bf16[1,128,3584]{2,1,0:T(8,128)(2,1)S(1)}, bf16[1,128,3584]{2,1,0:T(8,128)(2,1)}, u32[]{:S(2)}) copy-start(bf16[1,128,3584]{2,1,0:T(8,128)(2,1)} %get-tuple-element.9) | copy-start | bytes 2752516
  827.8 10.5 %copy-start.10 = (bf16[1,128,3584]{2,1,0:T(8,128)(2,1)S(1)}, bf16[1,128,3584]{2,1,0:T(8,128)(2,1)}, u32[]{:S(2)}) copy-start(bf16[1,128,3584]{2,1,0:T(8,128)(2,1)} %get-tuple-element.10) | copy-start | bytes 2752516
  (6 other events, 25.8 us)
Sparse Core Ops, SparseCore 0:
  10.3 47.4 all-gather.12
  60.1 45.2 all-gather.14
  107.7 45.2 all-gather.16
  155.0 45.2 all-gather.20
  202.4 45.2 all-gather.22
  249.8 45.2 all-gather.18
  413.0 47.6 reduce-scatter.14
  463.1 47.1 reduce-scatter.16
  512.7 47.1 reduce-scatter.10
  562.2 47.1 reduce-scatter.12
  611.8 47.1 reduce-scatter.6
  661.3 47.1 reduce-scatter.8
  712.8 114.9 all-reduce.2
where the time goes:
time: 864 us; the launch traced here: 856 us
  matrix products  396 us (46%)
  waiting for transfers between devices  392 us (45%)
  other arithmetic  26.9 us (3%)
  local copies, waits for them, and re-layouts  25.5 us (3%)
  between operations  14.3 us (2%)
    dot_general x5, matrix products, layer(): gate = jnp.dot(a, w['w_gate'], preferred_element_type=jnp.float32)  146 us
    reduce_scatter x6, waiting for transfers between devices, summed(): lax.psum_scatter(term, 's', scatter_dimension=0, tiled=True)  137 us
    dot_general x5, matrix products, layer(): up = jnp.dot(a, w['w_up'], preferred_element_type=jnp.float32)  136 us
    all_gather x6, waiting for transfers between devices, fetched(): lax.all_gather(w[number], 's', axis=0, tiled=True)  134 us
    psum x1, waiting for transfers between devices, summed(): lax.psum(lax.psum_scatter(term, 's', scatter_dimension=0, tiled=True), 'r')  119 us
    dot_general x5, matrix products, matmul(): jnp.dot(a, w, preferred_element_type=jnp.float32).astype(jnp.bfloat16)  115 us
    convert_element_type x2, other arithmetic, adamw(): return ((w - 0.02 * step).astype(jnp.bfloat16), m, v)  19 us
    unnamed x36, local copies, waits for them, and re-layouts  18.4 us
  transfers between devices with their start and end apart: 13, of which 10 were waited for; matrix products, arithmetic and copies ran while one was open for 36% of the time, Pallas kernels for 0%

commit v1 on v0

v1 whole, which is shorter than its diff:
```python
import functools

import jax
import jax.numpy as jnp
from jax import lax
from jax.experimental import pallas as pl
from jax.experimental.pallas import tpu as pltpu
from jax.sharding import PartitionSpec as P

BF, F32 = jnp.bfloat16, jnp.float32
MIB = 1 << 20
TOKENS, D, FF = 2048, 1024, 3584
TN = 512
MESH = pl.DeviceIdType.MESH

NN = (((1,), (0,)), ((), ()))
NT = (((1,), (1,)), ((), ()))
TNN = (((0,), (0,)), ((), ()))


def dot(a, b, dims=NN):
    return lax.dot_general(a, b, dims, preferred_element_type=F32)


def params(**kw):
    return pltpu.CompilerParams(vmem_limit_bytes=60 * MIB, **kw)


def cost(flops, nbytes):
    return pl.CostEstimate(flops=flops, bytes_accessed=nbytes, transcendentals=0)


def normed(h):
    wide = h.astype(F32)
    scale = lax.rsqrt(jnp.mean(wide**2, -1, keepdims=True) + 1e-6)
    return (wide * scale).astype(BF)


def adamw(w, m, v, g):
    m = 0.9 * m + 0.1 * g
    v = 0.95 * v + 0.05 * g * g
    step = m * lax.rsqrt(v + 1e-8) + 0.1 * w
    return (w - 0.02 * step).astype(BF), m, v


def split_rows(rows, chunk):
    return [pl.ds(i * chunk, chunk) for i in range(rows // chunk)]


def gate_up_kernel(a_ref, wg_ref, wu_ref, hid_ref, gate_ref, up_ref):
    for rows in split_rows(a_ref.shape[0], 256):
        a = a_ref[rows, :]
        gate, up = dot(a, wg_ref[...]), dot(a, wu_ref[...])
        gate_ref[rows, :] = gate
        up_ref[rows, :] = up
        hid_ref[rows, :] = (gate * jax.nn.sigmoid(gate) * up).astype(BF)


def gate_up(a, w, first):
    tm, at = 1024, first * (FF // TN)
    tile = pl.BlockSpec((tm, TN), lambda j, i: (i, j))
    return pl.pallas_call(
        gate_up_kernel,
        grid=(FF // TN, TOKENS // tm),
        in_specs=[
            pl.BlockSpec((tm, D), lambda j, i: (i, 0)),
            pl.BlockSpec((D, TN), lambda j, i: (0, at + j)),
            pl.BlockSpec((D, TN), lambda j, i: (0, at + FF // TN + j)),
        ],
        out_specs=[tile, tile, tile],
        out_shape=[jax.ShapeDtypeStruct((TOKENS, FF), t) for t in (BF, F32, F32)],
        compiler_params=params(),
        cost_estimate=cost(4 * TOKENS * D * FF, 100 * MIB),
        name="gate_up",
    )(a, w, w)


def grads_of_act(gate, up, d_hidden):
    sig = jax.nn.sigmoid(gate)
    silu = gate * sig
    d = d_hidden.astype(BF).astype(F32)
    return silu * up, d * up * (sig + silu * (1.0 - sig)), d * silu


def last_layer_kernel(a_ref, dy_ref, wg_ref, wu_ref, wd_ref, hid_ref, dg_ref, du_ref):
    for rows in split_rows(a_ref.shape[0], 256):
        a = a_ref[rows, :]
        gate, up = dot(a, wg_ref[...]), dot(a, wu_ref[...])
        hid, dg, du = grads_of_act(gate, up, dot(dy_ref[rows, :], wd_ref[...], NT))
        hid_ref[rows, :] = hid.astype(BF)
        dg_ref[rows, :] = dg.astype(BF)
        du_ref[rows, :] = du.astype(BF)


def last_layer(a, dy, w, first, wd):
    tm, at = 1024, first * (FF // TN)
    tile = pl.BlockSpec((tm, TN), lambda j, i: (i, j))
    wide = pl.BlockSpec((tm, D), lambda j, i: (i, 0))
    return pl.pallas_call(
        last_layer_kernel,
        grid=(FF // TN, TOKENS // tm),
        in_specs=[
            wide,
            wide,
            pl.BlockSpec((D, TN), lambda j, i: (0, at + j)),
            pl.BlockSpec((D, TN), lambda j, i: (0, at + FF // TN + j)),
            pl.BlockSpec((TN, D), lambda j, i: (j, 0)),
        ],
        out_specs=[tile, tile, tile],
        out_shape=[jax.ShapeDtypeStruct((TOKENS, FF), BF)] * 3,
        compiler_params=params(),
        cost_estimate=cost(6 * TOKENS * D * FF, 80 * MIB),
        name="last_layer",
    )(a, dy, w, w, wd)


def act_grad_kernel(dh_ref, wd_ref, gate_ref, up_ref, dg_ref, du_ref):
    for rows in split_rows(dh_ref.shape[0], 256):
        _, dg, du = grads_of_act(gate_ref[rows, :], up_ref[rows, :], dot(dh_ref[rows, :], wd_ref[...], NT))
        dg_ref[rows, :] = dg.astype(BF)
        du_ref[rows, :] = du.astype(BF)


def act_grad(dh, wd, gate, up):
    tm = 1024
    tile = pl.BlockSpec((tm, TN), lambda j, i: (i, j))
    return pl.pallas_call(
        act_grad_kernel,
        grid=(FF // TN, TOKENS // tm),
        in_specs=[
            pl.BlockSpec((tm, D), lambda j, i: (i, 0)),
            pl.BlockSpec((TN, D), lambda j, i: (j, 0)),
            tile,
            tile,
        ],
        out_specs=[tile, tile],
        out_shape=[jax.ShapeDtypeStruct((TOKENS, FF), BF)] * 2,
        compiler_params=params(),
        cost_estimate=cost(2 * TOKENS * D * FF, 120 * MIB),
        name="act_grad",
    )(dh, wd, gate, up)


def norm_grad_kernel(dg_ref, du_ref, wg_ref, wu_ref, h_ref, dy_ref, dh_ref, acc):
    k = pl.program_id(1)
    both = dot(dg_ref[...], wg_ref[...], NT) + dot(du_ref[...], wu_ref[...], NT)

    @pl.when(k == 0)
    def _():
        acc[...] = both

    @pl.when(k > 0)
    def _():
        acc[...] += both

    @pl.when(k == pl.num_programs(1) - 1)
    def _():
        @pl.loop(0, acc.shape[0] // 128)
        def _(i):
            rows = pl.ds(pl.multiple_of(i * 128, 128), 128)
            da = acc[rows, :].astype(BF).astype(F32)
            wide = h_ref[rows, :].astype(F32)
            scale = lax.rsqrt(jnp.mean(wide * wide, -1, keepdims=True) + 1e-6)
            along = jnp.mean(da * wide, -1, keepdims=True)
            dh = (da * scale - wide * (scale * scale * scale * along)).astype(BF)
            dh_ref[rows, :] = dy_ref[rows, :] + dh


def norm_grad(dg, du, w, first, h, dy):
    tm, at = 1024, first * (FF // TN)
    tile = pl.BlockSpec((tm, TN), lambda i, k: (i, k))
    wide = pl.BlockSpec((tm, D), lambda i, k: (i, 0))
    return pl.pallas_call(
        norm_grad_kernel,
        grid=(TOKENS // tm, FF // TN),
        in_specs=[
            tile,
            tile,
            pl.BlockSpec((D, TN), lambda i, k: (0, at + k)),
            pl.BlockSpec((D, TN), lambda i, k: (0, at + FF // TN + k)),
            wide,
            wide,
        ],
        out_specs=wide,
        out_shape=jax.ShapeDtypeStruct((TOKENS, D), BF),
        scratch_shapes=[pltpu.VMEM((tm, D), F32)],
        compiler_params=params(),
        cost_estimate=cost(4 * TOKENS * D * FF, 60 * MIB),
        name="norm_grad",
    )(dg, du, w, w, h, dy)


class Place:
    def __init__(self):
        r, s = lax.axis_index("r"), lax.axis_index("s")
        self.r, self.s = r, s
        self.y, self.z = lax.div(r, 4), lax.rem(r, 4)
        self.x, self.c = lax.div(s, 2), lax.rem(s, 2)

    def partner(self):
        return (0, self.r, self.x * 2 + 1 - self.c)

    def along(self, axis, k):
        here = getattr(self, axis)
        there = lax.rem(here + k, 4)
        at = {"x": self.x, "y": self.y, "z": self.z, axis: there}
        return there, (0, at["y"] * 4 + at["z"], at["x"] * 2 + self.c)


def all_greet(me):
    barrier = pltpu.get_barrier_semaphore()
    peers = [me.partner()] + [me.along(axis, k)[1] for axis in "xyz" for k in (1, 2, 3)]
    for peer in peers:
        pl.semaphore_signal(barrier, inc=1, device_id=peer, device_id_type=MESH)
    pl.semaphore_wait(barrier, len(peers))


class Summed:
    def __init__(self, me, own, core, away, buffers, sems, out):
        self.me, self.own, self.core, self.away, self.out = me, own, core, away, out
        self.from_core, self.first, self.second, self.third = buffers
        self.send, self.recv, self.local = sems
        self.rows, self.cols = out.shape
        self.part, self.half = self.rows // 4, self.cols // 2
        self.flying = []

    def piece(self, color, where):
        rows = pl.ds(pl.multiple_of(where * self.part, self.part), self.part)
        return rows, pl.ds(color * self.half, self.half)

    def copy(self, stage, color, k, src, dst, device):
        one = pltpu.make_async_remote_copy(
            src_ref=src,
            dst_ref=dst,
            send_sem=self.send.at[stage, color, k],
            recv_sem=self.recv.at[stage, color, k],
            device_id=device,
            device_id_type=MESH,
        )
        return one

    def copies(self, stage):
        me = self.me
        if stage == 0:
            return [self.copy(0, 0, 0, self.away, self.from_core, me.partner())]
        made = []
        for color in (0, 1):
            main, other = ("y", "z") if color == 0 else ("z", "y")
            mine = getattr(me, main)
            for k in (1, 2, 3):
                if stage == 1:
                    there, device = me.along(main, k)
                    rows, cols = self.piece(color, there)
                    src, dst = self.own.at[:, self.core, rows, cols], self.first.at[color, k - 1]
                elif stage == 2:
                    there, device = me.along("x", k)
                    rows, cols = self.piece(color, mine)
                    src, dst = self.own.at[there, self.core, rows, cols], self.second.at[color, k - 1]
                elif stage == 3:
                    _, device = me.along(other, k)
                    rows, cols = self.piece(color, mine)
                    src, dst = self.own.at[me.x, self.core, rows, cols], self.third.at[color, getattr(me, other)]
                else:
                    _, device = me.along(main, k)
                    rows, cols = self.piece(color, mine)
                    src, dst = self.own.at[me.x, self.core, rows, cols], self.out.at[rows, cols]
                made.append(self.copy(stage, color, k - 1, src, dst, device))
        return made

    def locals_(self):
        made = []
        for color in (0, 1):
            rows, cols = self.piece(color, self.me.y if color == 0 else self.me.z)
            src = self.own.at[self.me.x, self.core, rows, cols]
            made.append(pltpu.make_async_copy(src, self.out.at[rows, cols], self.local.at[color]))
        return made

    def start(self, stage):
        me = self.me
        if stage == 3:
            for color in (0, 1):
                rows, cols = self.piece(color, me.y if color == 0 else me.z)
                self.third[color, me.z if color == 0 else me.y] = self.own[me.x, self.core, rows, cols]
        for one in self.copies(stage):
            one.start()
        if stage == 4:
            for one in self.locals_():
                one.start()

    def finish(self, stage):
        me, own, core = self.me, self.own, self.core
        for one in self.copies(stage):
            one.wait()
        if stage == 0:
            step = 32 if self.rows % 64 else 64
            step = 32 if self.cols > 1024 else step

            @pl.loop(0, 4)
            def _(x):
                @pl.loop(0, self.rows // step)
                def _(i):
                    rows = pl.ds(pl.multiple_of(i * step, step), step)
                    own[x, core, rows, :] = (own[x, core, rows, :].astype(F32) + self.from_core[x, rows, :].astype(F32)).astype(BF)

        elif stage == 1:
            for color in (0, 1):
                rows, cols = self.piece(color, me.y if color == 0 else me.z)

                @pl.loop(0, 4)
                def _(x, color=color, rows=rows, cols=cols):
                    total = own[x, core, rows, cols].astype(F32)
                    for k in range(3):
                        total += self.first[color, k, x].astype(F32)
                    own[x, core, rows, cols] = total.astype(BF)

        elif stage == 2:
            for color in (0, 1):
                rows, cols = self.piece(color, me.y if color == 0 else me.z)
                total = own[me.x, core, rows, cols].astype(F32)
                for k in range(3):
                    total += self.second[color, k].astype(F32)
                own[me.x, core, rows, cols] = total.astype(BF)
        elif stage == 3:
            for color in (0, 1):
                rows, cols = self.piece(color, me.y if color == 0 else me.z)
                total = self.third[color, 0].astype(F32)
                for k in range(1, 4):
                    total += self.third[color, k].astype(F32)
                own[me.x, core, rows, cols] = total.astype(BF)
        else:
            for one in self.locals_():
                one.wait()


def buffers_of(rows, cols):
    part, half = rows // 4, cols // 2
    return [
        pltpu.VMEM((4, rows, cols), BF),
        pltpu.VMEM((2, 3, 4, part, half), BF),
        pltpu.VMEM((2, 3, part, half), BF),
        pltpu.VMEM((2, 4, part, half), BF),
    ]


def sems_of():
    return [pltpu.SemaphoreType.DMA((5, 2, 3)), pltpu.SemaphoreType.DMA((5, 2, 3)), pltpu.SemaphoreType.DMA((2,))]


def first_layer_kernel(a_ref, dg_ref, du_ref, down_ref, gd_ref, gg_ref, gu_ref, own_d, term_g, term_u, load, *rest):
    i = pl.program_id(0)
    steps = FF // TN
    me = Place()
    parts = [(rest[7 * n : 7 * n + 4], rest[7 * n + 4 : 7 * n + 7]) for n in range(3)]
    down = Summed(me, own_d, 0, down_ref.at[:, 1 - me.c], *parts[0], gd_ref)
    gate = Summed(me, term_g, me.c, term_g.at[:, 1 - me.c], *parts[1], gg_ref)
    up = Summed(me, term_u, me.c, term_u.at[:, 1 - me.c], *parts[2], gu_ref)
    loading = pltpu.make_async_copy(down_ref.at[:, me.c], own_d.at[:, 0], load)

    @pl.when(i == 0)
    def _():
        all_greet(me)
        down.start(0)
        loading.start()

    for term, d_ref, first in ((term_g, dg_ref, 0), (term_u, du_ref, steps)):

        @pl.when(jnp.logical_and(i >= first, i < first + steps))
        def _(term=term, d_ref=d_ref, first=first):
            cols = pl.ds(pl.multiple_of((i - first) * TN, TN), TN)
            term[:, :, :, cols] = dot(a_ref[...], d_ref[...], TNN).astype(BF).reshape(4, 2, D // 8, TN)

    @pl.when(i == 2)
    def _():
        loading.wait()
        down.finish(0)
        down.start(1)

    @pl.when(i == steps - 1)
    def _():
        gate.start(0)

    @pl.when(i == steps + 2)
    def _():
        gate.finish(0)

    @pl.when(i == steps + 3)
    def _():
        down.finish(1)
        down.start(2)
        gate.start(1)

    @pl.when(i == 2 * steps - 1)
    def _():
        up.start(0)
        down.finish(2)
        down.start(3)
        up.finish(0)
        down.finish(3)
        down.start(4)
        up.start(1)
        gate.finish(1)
        gate.start(2)
        gate.finish(2)
        gate.start(3)
        gate.finish(3)
        gate.start(4)
        up.finish(1)
        up.start(2)
        up.finish(2)
        up.start(3)
        up.finish(3)
        up.start(4)
        for one in (down, gate, up):
            one.finish(4)


def first_layer_grads(a, dg, du, down):
    steps = FF // TN
    rows_d, rows = FF // 8, D // 8
    anywhere = pl.BlockSpec(memory_space=pl.ANY)
    gd, gg, gu = pl.pallas_call(
        first_layer_kernel,
        grid=(2 * steps,),
        in_specs=[
            pl.BlockSpec((TOKENS, D), lambda i: (0, 0), pipeline_mode=pl.Buffered(1)),
            pl.BlockSpec((TOKENS, TN), lambda i: (0, jnp.minimum(i, steps - 1))),
            pl.BlockSpec((TOKENS, TN), lambda i: (0, jnp.maximum(i - steps, 0))),
            anywhere,
        ],
        out_specs=[anywhere] * 3,
        out_shape=[
            jax.ShapeDtypeStruct((rows_d, D), BF),
            jax.ShapeDtypeStruct((rows, FF), BF),
            jax.ShapeDtypeStruct((rows, FF), BF),
        ],
        scratch_shapes=[
            pltpu.VMEM((4, 1, rows_d, D), BF),
            pltpu.VMEM((4, 2, rows, FF), BF),
            pltpu.VMEM((4, 2, rows, FF), BF),
            pltpu.SemaphoreType.DMA,
            *buffers_of(rows_d, D),
            *sems_of(),
            *buffers_of(rows, FF),
            *sems_of(),
            *buffers_of(rows, FF),
            *sems_of(),
        ],
        compiler_params=pltpu.CompilerParams(
            vmem_limit_bytes=67_043_328,
            collective_id=0,
            has_side_effects=True,
        ),
        cost_estimate=cost(4 * TOKENS * D * FF, 60 * MIB),
        name="first_layer_grads",
    )(a, dg, du, down.reshape(4, 2, rows_d, D))
    return gg, gu, gd


def solution(mesh):
    def step(x, dy, *arrays):
        weights, m, v = (arrays[i : i + 3] for i in (0, 3, 6))
        x, dy = x[0], dy[0]
        place = lax.axis_index("r")
        rows = weights[0].shape[1] // 16
        mine = [lax.dynamic_slice_in_dim(weights[n][layer], place * rows, rows, 0) for layer in (0, 1) for n in (0, 1)]
        w = lax.all_gather(jnp.concatenate(mine, 1), ("s", "r"), axis=0, tiled=True)
        wd = [lax.all_gather(weights[2][layer], "s", axis=0, tiled=True) for layer in (0, 1)]

        a0 = normed(x)
        hid0, gate0, up0 = gate_up(a0, w, 0)
        h1 = x + dot(hid0, wd[0]).astype(BF)
        a1 = normed(h1)
        hid1, dg1, du1 = last_layer(a1, dy, w, 2, wd[1])

        def scattered(term):
            return lax.psum_scatter(term, "s", scatter_dimension=0, tiled=True)

        terms = [scattered(dot(a, b, TNN).astype(BF)) for a, b in ((hid1, dy), (a1, dg1), (a1, du1))]
        dh1 = norm_grad(dg1, du1, w, 2, h1, dy)
        down0 = dot(hid0, dh1, TNN).astype(BF)
        dg0, du0 = act_grad(dh1, wd[0], gate0, up0)
        d1, g1, u1 = (lax.psum(t, "r") for t in terms)
        g0, u0, d0 = first_layer_grads(a0, dg0, du0, down0)
        gradients = [jnp.stack(pair).astype(F32) for pair in ((g0, g1), (u0, u1), (d0, d1))]
        new = [adamw(w.astype(F32), m, v, g) for w, m, v, g in zip(weights, m, v, gradients, strict=True)]
        return tuple(one[which] for which in range(3) for one in new)

    states, cut = P(("rep", "r", "s"), None, None), P(None, "s", None)
    return jax.shard_map(
        step,
        mesh=mesh,
        in_specs=(states, states) + (cut,) * 9,
        out_specs=(P("rep", "s", None),) * 9,
        check_vma=False,
    )
```

time: 864 us -> 634 us (0.73)
  Pallas kernels: 0 us -> 352 us
  matrix products: 396 us -> 109 us
  waiting for transfers between devices: 392 us -> 107 us
  local copies, waits for them, and re-layouts: 25.5 us -> 14.6 us
    pallas_call x0 -> x5, Pallas kernels: none -> 352 us  [the longest x1 142 us: first_layer_grads(): pl.pallas_call(first_layer_kernel, grid=(2 * steps,), in_specs=[pl.BlockS...]
    dot_general x15 -> x5, matrix products: 396 us -> 109 us  [dot(): return lax.dot_general(a, b, dims, preferred_element_type=F32)]
    reduce_scatter x6 -> x3, waiting for transfers between devices: 137 us -> 0.01 us  [scattered(): return lax.psum_scatter(term, 's', scatter_dimension=0, tiled=True)]
    psum x1, waiting for transfers between devices: 119 us -> 0.02 us  [step(): d1, g1, u1 = (lax.psum(t, 'r') for t in terms)]
    all_gather x6 -> x3, waiting for transfers between devices: 134 us -> 106 us  [the longest x1 92.3 us: step(): w = lax.all_gather(jnp.concatenate(mine, 1), ('s', 'r'), axis=0, tiled=True)]
    unnamed x36 -> x26, local copies, waits for them, and re-layouts: 18.4 us -> 6.09 us
    convert_element_type x2 -> x5, other arithmetic: 19 us -> 23.9 us  [the longest x3 18.4 us: adamw(): return ((w - 0.02 * step).astype(BF), m, v)]
  transfers between devices with their start and end apart: 13 -> 7, of which waited for: 10 -> 2; matrix products, arithmetic and copies ran while one was open for 36% -> 16% of each run, Pallas kernels for 0% -> 47%
where the time goes in v1:
time: 634 us; the launch traced here: 625 us
  Pallas kernels  352 us (56%)
  matrix products  109 us (17%)
  waiting for transfers between devices  107 us (17%)
  other arithmetic  27.8 us (4%)
  local copies, waits for them, and re-layouts  14.6 us (2%)
  between operations  14.5 us (2%)
    pallas_call x1, Pallas kernels, first_layer_grads(): pl.pallas_call(first_layer_kernel, grid=(2 * steps,), in_specs=[pl.BlockS...  142 us
    dot_general x5, matrix products, dot(): return lax.dot_general(a, b, dims, preferred_element_type=F32)  109 us
    all_gather x1, waiting for transfers between devices, step(): w = lax.all_gather(jnp.concatenate(mine, 1), ('s', 'r'), axis=0, tiled=True)  92.3 us
    pallas_call x1, Pallas kernels, last_layer(): pl.pallas_call(last_layer_kernel, grid=(FF // TN, TOKENS // tm), in_specs...  59.7 us
    pallas_call x1, Pallas kernels, gate_up(): pl.pallas_call(gate_up_kernel, grid=(FF // TN, TOKENS // tm), in_specs=[p...  55.2 us
    pallas_call x1, Pallas kernels, norm_grad(): pl.pallas_call(norm_grad_kernel, grid=(TOKENS // tm, FF // TN), in_specs=...  48.5 us
    pallas_call x1, Pallas kernels, act_grad(): pl.pallas_call(act_grad_kernel, grid=(FF // TN, TOKENS // tm), in_specs=[...  47.1 us
    convert_element_type x3, other arithmetic, adamw(): return ((w - 0.02 * step).astype(BF), m, v)  18.4 us
  transfers between devices with their start and end apart: 7, of which 2 were waited for; matrix products, arithmetic and copies ran while one was open for 16% of the time, Pallas kernels for 47%

profile of v1, /device:TPU:0, one launch (start us, length us, event | category | flops | bytes accessed | tf_op | source)
XLA Modules:
  0.0 625.4 jit_solution(403766582707980895)
XLA Ops:
  7.2 2.9 fusion.28
  10.2 1.0 fusion.29
  13.7 2.8 fusion.27
  17.3 3.2 fusion
  20.8 2.8 fusion.1.a_ref
  23.5 92.3 %all-gather.6.cloned.1.call-done.wg_ref.wu_ref = bf16[1024,14336]{1,0:T(8,128)(2,1)} async-done(((bf16[8,14336]{1,0:T(8,128)(2,1)}), bf16[1024,14336]{1,0:T(8,128)(2,1)}) %all-gather.6.cloned.1.call-update) | async-done | bytes 29360144 | tf_op jit(solution)/shard_map/all_gather | solution.py:466
  115.8 55.2 %gate_up.1 = (bf16[2048,3584]{1,0:T(8,128)(2,1)}, f32[2048,3584]{1,0:T(8,128)}, f32[2048,3584]{1,0:T(8,128)}) custom-call(bf16[2048,1024]{1,0:T(8,128)(2,1)} %fusion.1.a_ref, bf16[1024,14336]{1,0:T(8,128)(2,1)} %all-gather.6.cloned.1.call-done.wg_ref.wu_ref, bf16[1024,14336]{1,0:T(8,128)(2,1)} %all-gather.6.cloned.1.call-done.wg_ref.wu_ref), custom_call_target="tpu_custom_call" | custom-call | flops 30064771072 | bytes 104857600 | tf_op jit(solution)/shard_map/gate_up/pallas_call | solution.py:62
  171.0 20.9 %fusion.2 = (f32[2048]{0:T(1024)S(1)}, bf16[2048,1024]{1,0:T(8,128)(2,1)S(1)}) fusion(bf16[2048,3584]{1,0:T(8,128)(2,1)} %get-tuple-element.20, bf16[1,3584,1024]{2,1,0:T(8,128)(2,1)} %all-gather.8.cloned.1.call-done, bf16[1,2048,1024]{2,1,0:T(8,128)(2,1)} %param.11), kind=kOutput, calls=%fused_computation.6 | convolution fusion | flops 15042869248 | bytes 30416896 | tf_op jit(solution)/shard_map/dot_general | solution.py:22
  191.9 1.9 copy-done.4
  193.8 2.7 fusion.3.a_ref
  196.5 13.5 %all-gather.10.cloned.1.call-done = bf16[1,3584,1024]{2,1,0:T(8,128)(2,1)} async-done(((bf16[1,448,1024]{2,1,0:T(8,128)(2,1)}), bf16[1,3584,1024]{2,1,0:T(8,128)(2,1)}) %all-gather.10.cloned.1.call-update) | async-done | bytes 7340048 | tf_op jit(solution)/shard_map/all_gather | solution.py:467
  210.0 59.7 %last_layer.1 = (bf16[2048,3584]{1,0:T(8,128)(2,1)}, bf16[2048,3584]{1,0:T(8,128)(2,1)}, bf16[2048,3584]{1,0:T(8,128)(2,1)}) custom-call(bf16[2048,1024]{1,0:T(8,128)(2,1)} %fusion.3.a_ref, bf16[2048,1024]{1,0:T(8,128)(2,1)} %bitcast.44, bf16[1024,14336]{1,0:T(8,128)(2,1)} %all-gather.6.cloned.1.call-done.wg_ref.wu_ref, ...), custom_call_target="tpu_custom_call" | custom-call | flops 45097156608 | bytes 83886080 | tf_op jit(solution)/shard_map/last_layer/pallas_call | solution.py:99
  269.8 22.3 %convolution_convert_fusion = bf16[3584,1024]{1,0:T(8,128)(2,1)} fusion(bf16[2048,3584]{1,0:T(8,128)(2,1)} %get-tuple-element.30, bf16[1,2048,1024]{2,1,0:T(8,128)(2,1)} %param.12), kind=kOutput, calls=%fused_computation.8 | convolution fusion | flops 15036055552 | bytes 26214400 | tf_op jit(solution)/shard_map/dot_general | solution.py:22
  292.2 22.2 %convolution_convert_fusion.1 = bf16[1024,3584]{1,0:T(8,128)(2,1)} fusion(bf16[2048,1024]{1,0:T(8,128)(2,1)} %fusion.3.a_ref, bf16[2048,3584]{1,0:T(8,128)(2,1)} %get-tuple-element.22.du_ref), kind=kOutput, calls=%fused_computation.9 | convolution fusion | flops 15036055552 | bytes 26214400 | tf_op jit(solution)/shard_map/dot_general | solution.py:22
  314.5 22.3 %convolution_convert_fusion.2 = bf16[1024,3584]{1,0:T(8,128)(2,1)} fusion(bf16[2048,1024]{1,0:T(8,128)(2,1)} %fusion.3.a_ref, bf16[2048,3584]{1,0:T(8,128)(2,1)} %get-tuple-element.21.dg_ref), kind=kOutput, calls=%fused_computation.10 | convolution fusion | flops 15036055552 | bytes 26214400 | tf_op jit(solution)/shard_map/dot_general | solution.py:22
  336.8 48.5 %norm_grad.1.dh_ref = bf16[2048,1024]{1,0:T(8,128)(2,1)} custom-call(bf16[2048,3584]{1,0:T(8,128)(2,1)} %get-tuple-element.21.dg_ref, bf16[2048,3584]{1,0:T(8,128)(2,1)} %get-tuple-element.22.du_ref, bf16[1024,14336]{1,0:T(8,128)(2,1)} %all-gather.6.cloned.1.call-done.wg_ref.wu_ref, bf16[1024,14336]{1,0:T(8,128)(2,1)} %all-gather.6.cloned.1.call-done.wg_ref.wu_ref, ...), custom_call_target="tpu_custom_call" | custom-call | flops 30064771072 | bytes 62914560 | tf_op jit(solution)/shard_map/norm_grad/pallas_call | solution.py:173
  385.3 47.1 %act_grad.1 = (bf16[2048,3584]{1,0:T(8,128)(2,1)}, bf16[2048,3584]{1,0:T(8,128)(2,1)}) custom-call(bf16[2048,1024]{1,0:T(8,128)(2,1)} %norm_grad.1.dh_ref, bf16[3584,1024]{1,0:T(8,128)(2,1)} %bitcast.36, f32[2048,3584]{1,0:T(8,128)} %get-tuple-element.23.gate_ref, f32[2048,3584]{1,0:T(8,128)} %get-tuple-element.24.up_ref), custom_call_target="tpu_custom_call" | custom-call | flops 15032385536 | bytes 125829120 | tf_op jit(solution)/shard_map/act_grad/pallas_call | solution.py:127
  432.4 21.8 %convolution_convert_fusion.3 = bf16[3584,1024]{1,0:T(8,128)(2,1)} fusion(bf16[2048,3584]{1,0:T(8,128)(2,1)} %get-tuple-element.20, bf16[2048,1024]{1,0:T(8,128)(2,1)} %norm_grad.1.dh_ref), kind=kOutput, calls=%fused_computation.11 | convolution fusion | flops 15036055552 | bytes 26214400 | tf_op jit(solution)/shard_map/dot_general | solution.py:22
  454.2 141.8 %first_layer_grads.1 = (bf16[448,1024]{1,0:T(8,128)(2,1)}, bf16[128,3584]{1,0:T(8,128)(2,1)}, bf16[128,3584]{1,0:T(8,128)(2,1)}) custom-call(bf16[2048,1024]{1,0:T(8,128)(2,1)} %fusion.1.a_ref, bf16[2048,3584]{1,0:T(8,128)(2,1)} %get-tuple-element.25.dg_ref, bf16[2048,3584]{1,0:T(8,128)(2,1)} %get-tuple-element.26.du_ref, bf16[4,2,448,1024]{3,2,1,0:T(8,128)(2,1)} %bitcast.46), custom_call_target="tpu_custom_call" | custom-call | flops 30064771072 | bytes 62914560 | tf_op jit(solution)/shard_map/first_layer_grads/pallas_call | solution.py:421
  596.1 8.3 %fusion.6 = (bf16[2,128,3584]{2,1,0:T(8,128)(2,1)}, f32[2,128,3584]{2,1,0:T(8,128)}, f32[2,128,3584]{2,1,0:T(8,128)}) fusion(bf16[2,128,3584]{2,1,0:T(8,128)(2,1)} %param.13, bf16[1,128,3584]{2,1,0:T(8,128)(2,1)} %get-tuple-element.31, bf16[1,128,3584]{2,1,0:T(8,128)(2,1)} %bitcast.42, f32[2,128,3584]{2,1,0:T(8,128)} %param.19, f32[2,128,3584]{2,1,0:T(8,128)} %param.16), kind=kLoop, calls=%fused_computation.27 | loop fusion | flops 17432576 | bytes 20185088 | tf_op jit(solution)/shard_map/convert_element_type | solution.py:43
  604.4 1.8 copy-done.6
  606.6 5.5 fusion.10
  612.1 1.3 copy-done.8
  613.8 4.6 fusion.14
  (47 shorter events, 4.6 us)
Async XLA Ops:
  7.2 3.0 copy-start.1
  7.2 108.6 %all-gather.6.cloned.1.call-start = ((), (), s32[]{:S(2)}) async-start(), calls=%async_computation.3 | async-start | bytes 29589504 | tf_op jit(solution)/shard_map/all_gather | solution.py:466
  13.6 157.4 %all-gather.8.cloned.1.call-start = ((), (), s32[]{:S(2)}) async-start(), calls=%async_computation.7 | async-start | bytes 8257536 | tf_op jit(solution)/shard_map/all_gather | solution.py:467
  16.5 193.5 %all-gather.10.cloned.1.call-start = ((), (), s32[]{:S(2)}) async-start(), calls=%async_computation.8 | async-start | bytes 8257536 | tf_op jit(solution)/shard_map/all_gather | solution.py:467
  17.3 436.9 %reduce-scatter.8.cloned.1.call-start = ((), (), s32[]{:S(2)}) async-start(), calls=%async_computation.6 | async-start | bytes 8257536 | tf_op jit(solution)/shard_map/reduce_scatter | solution.py:476
  17.3 3.5 copy-start
  191.9 1.9 copy-start.4
  292.1 162.1 %reduce-scatter.6.cloned.1.call-start = ((), (), s32[]{:S(2)}) async-start(), calls=%async_computation.5 | async-start | bytes 8257536 | tf_op jit(solution)/shard_map/reduce_scatter | solution.py:476
  314.4 139.8 %reduce-scatter.4.cloned.1.call-start = ((), (), s32[]{:S(2)}) async-start(), calls=%async_computation.4 | async-start | bytes 8257536 | tf_op jit(solution)/shard_map/reduce_scatter | solution.py:476
  336.7 259.3 %all-reduce.3.cloned.1.call-start = ((), (), s32[]{:S(2)}) async-start(), calls=%async_computation.9 | async-start | bytes 5505024 | tf_op jit(solution)/shard_map/psum | solution.py:482
  596.0 8.3 %copy-start.2 = (bf16[2,128,3584]{2,1,0:T(8,128)(2,1)S(1)}, bf16[2,128,3584]{2,1,0:T(8,128)(2,1)}, u32[]{:S(2)}) copy-start(bf16[2,128,3584]{2,1,0:T(8,128)(2,1)} %param.14) | copy-start | bytes 5505028
  596.0 8.3 %copy-start.5 = (f32[2,128,3584]{2,1,0:T(8,128)S(1)}, f32[2,128,3584]{2,1,0:T(8,128)}, u32[]{:S(2)}) copy-start(f32[2,128,3584]{2,1,0:T(8,128)} %param.20) | copy-start | bytes 11010052
  596.1 10.1 %copy-start.6 = (f32[2,128,3584]{2,1,0:T(8,128)S(1)}, f32[2,128,3584]{2,1,0:T(8,128)}, u32[]{:S(2)}) copy-start(f32[2,128,3584]{2,1,0:T(8,128)} %param.17) | copy-start | bytes 11010052
  596.1 10.2 %copy-start.10 = (bf16[1,128,3584]{2,1,0:T(8,128)(2,1)S(1)}, bf16[1,128,3584]{2,1,0:T(8,128)(2,1)}, u32[]{:S(2)}) copy-start(bf16[1,128,3584]{2,1,0:T(8,128)(2,1)} %get-tuple-element.32) | copy-start | bytes 2752516
  596.1 10.5 %copy-start.12 = (bf16[128,3584]{1,0:T(8,128)(2,1)S(1)}, bf16[128,3584]{1,0:T(8,128)(2,1)}, u32[]{:S(2)}) copy-start(bf16[128,3584]{1,0:T(8,128)(2,1)} %get-tuple-element.28) | copy-start | bytes 2752516
  606.5 5.5 copy-start.3
  606.5 5.5 copy-start.7
  606.5 6.9 %copy-start.8 = (f32[2,448,1024]{2,1,0:T(8,128)S(1)}, f32[2,448,1024]{2,1,0:T(8,128)}, u32[]{:S(2)}) copy-start(f32[2,448,1024]{2,1,0:T(8,128)} %param.18) | copy-start | bytes 11010052
  606.6 7.0 %copy-start.9 = (bf16[1,448,1024]{2,1,0:T(8,128)(2,1)S(1)}, bf16[1,448,1024]{2,1,0:T(8,128)(2,1)}, u32[]{:S(2)}) copy-start(bf16[1,448,1024]{2,1,0:T(8,128)(2,1)} %get-tuple-element.33) | copy-start | bytes 2752516
  606.6 7.3 %copy-start.11 = (bf16[448,1024]{1,0:T(8,128)(2,1)S(1)}, bf16[448,1024]{1,0:T(8,128)(2,1)}, u32[]{:S(2)}) copy-start(bf16[448,1024]{1,0:T(8,128)(2,1)} %get-tuple-element.29) | copy-start | bytes 2752516
Sparse Core Ops, SparseCore 0:
  13.7 102.0 all-gather.5
  118.1 44.3 all-gather.7
  164.8 45.2 all-gather.9
  292.2 47.6 reduce-scatter.7
  342.2 47.1 reduce-scatter.5
  391.7 47.1 reduce-scatter.3
  454.3 135.8 all-reduce.2

commit v2 on v1

--- a/solution.py
+++ b/solution.py
@@ -45,34 +45,6 @@
 
 def split_rows(rows, chunk):
     return [pl.ds(i * chunk, chunk) for i in range(rows // chunk)]
-
-
-def gate_up_kernel(a_ref, wg_ref, wu_ref, hid_ref, gate_ref, up_ref):
-    for rows in split_rows(a_ref.shape[0], 256):
-        a = a_ref[rows, :]
-        gate, up = dot(a, wg_ref[...]), dot(a, wu_ref[...])
-        gate_ref[rows, :] = gate
-        up_ref[rows, :] = up
-        hid_ref[rows, :] = (gate * jax.nn.sigmoid(gate) * up).astype(BF)
-
-
-def gate_up(a, w, first):
-    tm, at = 1024, first * (FF // TN)
-    tile = pl.BlockSpec((tm, TN), lambda j, i: (i, j))
-    return pl.pallas_call(
-        gate_up_kernel,
-        grid=(FF // TN, TOKENS // tm),
-        in_specs=[
-            pl.BlockSpec((tm, D), lambda j, i: (i, 0)),
-            pl.BlockSpec((D, TN), lambda j, i: (0, at + j)),
-            pl.BlockSpec((D, TN), lambda j, i: (0, at + FF // TN + j)),
-        ],
-        out_specs=[tile, tile, tile],
-        out_shape=[jax.ShapeDtypeStruct((TOKENS, FF), t) for t in (BF, F32, F32)],
-        compiler_params=params(),
-        cost_estimate=cost(4 * TOKENS * D * FF, 100 * MIB),
-        name="gate_up",
-    )(a, w, w)
 
 
 def grads_of_act(gate, up, d_hidden):
@@ -92,19 +64,19 @@
         du_ref[rows, :] = du.astype(BF)
 
 
-def last_layer(a, dy, w, first, wd):
-    tm, at = 1024, first * (FF // TN)
-    tile = pl.BlockSpec((tm, TN), lambda j, i: (i, j))
-    wide = pl.BlockSpec((tm, D), lambda j, i: (i, 0))
+def last_layer(a, dy, w, wd):
+    tn = 256
+    tile = pl.BlockSpec((TOKENS, tn), lambda j: (0, j))
+    wide = pl.BlockSpec((TOKENS, D), lambda j: (0, 0), pipeline_mode=pl.Buffered(1))
     return pl.pallas_call(
         last_layer_kernel,
-        grid=(FF // TN, TOKENS // tm),
+        grid=(FF // tn,),
         in_specs=[
             wide,
             wide,
-            pl.BlockSpec((D, TN), lambda j, i: (0, at + j)),
-            pl.BlockSpec((D, TN), lambda j, i: (0, at + FF // TN + j)),
-            pl.BlockSpec((TN, D), lambda j, i: (j, 0)),
+            pl.BlockSpec((D, tn), lambda j: (0, j)),
+            pl.BlockSpec((D, tn), lambda j: (0, FF // tn + j)),
+            pl.BlockSpec((tn, D), lambda j: (j, 0)),
         ],
         out_specs=[tile, tile, tile],
         out_shape=[jax.ShapeDtypeStruct((TOKENS, FF), BF)] * 3,
@@ -114,22 +86,21 @@
     )(a, dy, w, w, wd)
 
 
-def act_grad_kernel(dh_ref, wd_ref, gate_ref, up_ref, dg_ref, du_ref):
+def act_grad_kernel(dh_ref, wd_ref, by_gate_ref, by_up_ref, dg_ref, du_ref):
     for rows in split_rows(dh_ref.shape[0], 256):
-        _, dg, du = grads_of_act(gate_ref[rows, :], up_ref[rows, :], dot(dh_ref[rows, :], wd_ref[...], NT))
-        dg_ref[rows, :] = dg.astype(BF)
-        du_ref[rows, :] = du.astype(BF)
-
-
-def act_grad(dh, wd, gate, up):
-    tm = 1024
-    tile = pl.BlockSpec((tm, TN), lambda j, i: (i, j))
+        d = dot(dh_ref[rows, :], wd_ref[...], NT).astype(BF).astype(F32)
+        dg_ref[rows, :] = (d * by_gate_ref[rows, :]).astype(BF)
+        du_ref[rows, :] = (d * by_up_ref[rows, :]).astype(BF)
+
+
+def act_grad(dh, wd, by_gate, by_up):
+    tile = pl.BlockSpec((TOKENS, TN), lambda j: (0, j))
     return pl.pallas_call(
         act_grad_kernel,
-        grid=(FF // TN, TOKENS // tm),
+        grid=(FF // TN,),
         in_specs=[
-            pl.BlockSpec((tm, D), lambda j, i: (i, 0)),
-            pl.BlockSpec((TN, D), lambda j, i: (j, 0)),
+            pl.BlockSpec((TOKENS, D), lambda j: (0, 0), pipeline_mode=pl.Buffered(1)),
+            pl.BlockSpec((TN, D), lambda j: (j, 0)),
             tile,
             tile,
         ],
@@ -138,7 +109,7 @@
         compiler_params=params(),
         cost_estimate=cost(2 * TOKENS * D * FF, 120 * MIB),
         name="act_grad",
-    )(dh, wd, gate, up)
+    )(dh, wd, by_gate, by_up)
 
 
 def norm_grad_kernel(dg_ref, du_ref, wg_ref, wu_ref, h_ref, dy_ref, dh_ref, acc):
@@ -166,8 +137,8 @@
             dh_ref[rows, :] = dy_ref[rows, :] + dh
 
 
-def norm_grad(dg, du, w, first, h, dy):
-    tm, at = 1024, first * (FF // TN)
+def norm_grad(dg, du, w, h, dy):
+    tm = 1024
     tile = pl.BlockSpec((tm, TN), lambda i, k: (i, k))
     wide = pl.BlockSpec((tm, D), lambda i, k: (i, 0))
     return pl.pallas_call(
@@ -176,8 +147,8 @@
         in_specs=[
             tile,
             tile,
-            pl.BlockSpec((D, TN), lambda i, k: (0, at + k)),
-            pl.BlockSpec((D, TN), lambda i, k: (0, at + FF // TN + k)),
+            pl.BlockSpec((D, TN), lambda i, k: (0, k)),
+            pl.BlockSpec((D, TN), lambda i, k: (0, FF // TN + k)),
             wide,
             wide,
         ],
@@ -213,6 +184,238 @@
     for peer in peers:
         pl.semaphore_signal(barrier, inc=1, device_id=peer, device_id_type=MESH)
     pl.semaphore_wait(barrier, len(peers))
+
+
+GROUPS = ((0, 1), (1, 1), (2, 1), (3, 2), (5, 2))
+
+
+class Gathered:
+    def __init__(self, me, w, number, sems):
+        self.me, self.number = me, number
+        self.send, self.recv = sems
+        first, count = GROUPS[number]
+        self.w = w.at[pl.ds(first, count)]
+
+    def rows(self, color):
+        quarter = D // 64
+        where = self.me.y if color == 0 else self.me.z
+        return pl.ds(pl.multiple_of((color * 4 + where) * quarter, quarter), quarter)
+
+    def copies(self, stage):
+        me, w, made = self.me, self.w, []
+
+        def copy(src, dst, color, k, device):
+            at = (self.number, stage, color, k)
+            made.append(pltpu.make_async_remote_copy(src_ref=src, dst_ref=dst, send_sem=self.send.at[at], recv_sem=self.recv.at[at], device_id=device, device_id_type=MESH))
+
+        if stage == 2:
+            copy(w.at[:, :, me.c], w.at[:, :, me.c], 0, 0, me.partner())
+            return made
+        for color in (0, 1):
+            rows = self.rows(color)
+            for k in (1, 2, 3):
+                if stage == 0:
+                    copy(w.at[:, 0, me.c, rows], w.at[:, 4 - k, me.c, rows], color, k - 1, me.along("x", k)[1])
+                else:
+                    others = w.at[:, pl.ds(1, 3), me.c, rows]
+                    copy(others, others, color, k - 1, me.along("yz"[color], k)[1])
+        return made
+
+    def start(self, stage):
+        for one in self.copies(stage):
+            one.start()
+
+    def finish(self, stage):
+        for one in self.copies(stage):
+            one.wait()
+
+
+class GatheredDown:
+    def __init__(self, me, own, out, held, sems):
+        self.me, self.own, self.out, self.held = me, own, out, held
+        self.send, self.recv, self.local = sems
+        self.part, self.half = own.shape[0] // 4, own.shape[1] // 2
+
+    def piece(self, color):
+        where = self.me.y if color == 0 else self.me.z
+        return pl.ds(pl.multiple_of(where * self.part, self.part), self.part), pl.ds(color * self.half, self.half)
+
+    def copies(self, stage):
+        me, out, made = self.me, self.out, []
+
+        def copy(src, dst, n, device):
+            at = (stage, n)
+            made.append(pltpu.make_async_remote_copy(src_ref=src, dst_ref=dst, send_sem=self.send.at[at], recv_sem=self.recv.at[at], device_id=device, device_id_type=MESH))
+
+        if stage == 2:
+            copy(self.own, out.at[me.x, me.c], 0, me.partner())
+            for k in (1, 2, 3):
+                x, _ = me.along("x", k)
+                copy(out.at[x, me.c], out.at[x, me.c], k, me.partner())
+            return made
+        for color in (0, 1):
+            rows, cols = self.piece(color)
+            for k in (1, 2, 3):
+                if stage == 0:
+                    copy(self.own.at[rows, cols], out.at[me.x, me.c, rows, cols], color * 3 + k - 1, me.along("x", k)[1])
+                    continue
+                for other in (1, 2, 3):
+                    there = out.at[me.along("x", other)[0], me.c, rows, cols]
+                    copy(there, there, (color * 3 + k - 1) * 3 + other - 1, me.along("yz"[color], k)[1])
+        return made
+
+    def taken(self):
+        return pltpu.make_async_copy(self.own, self.held, self.local.at[0])
+
+    def put(self):
+        return pltpu.make_async_copy(self.held, self.out.at[self.me.x, self.me.c], self.local.at[1])
+
+    def start(self, stage):
+        for one in self.copies(stage):
+            one.start()
+
+    def finish(self, stage):
+        for one in self.copies(stage):
+            one.wait()
+
+
+def first_layer_forward_kernel(x_ref, wg_ref, wu_ref, wd_ref, hid_ref, by_gate_ref, by_up_ref, wd0_ref, wd1_ref, w, a, held0, held1, load, *sems):
+    j = pl.program_id(0)
+    me = Place()
+    groups = [Gathered(me, w, n, sems[:2]) for n in range(len(GROUPS))]
+    downs = [GatheredDown(me, wd_ref.at[n], out, held, sems[2 + 3 * n : 5 + 3 * n]) for n, (out, held) in enumerate(((wd0_ref, held0), (wd1_ref, held1)))]
+    loads = []
+    for chunk in range(FF // TN):
+        for n, ref in enumerate((wg_ref, wu_ref)):
+            src = ref.at[0, :, pl.ds(chunk * TN, TN)]
+            loads.append(pltpu.make_async_copy(src, w.at[chunk, 0, me.c, :, pl.ds(n * TN, TN)], load.at[chunk, n]))
+
+    def onward(which, stage):
+        which.finish(stage)
+        which.start(stage + 1)
+
+    @pl.when(j == 0)
+    def _():
+        for one in loads:
+            one.start()
+        for down in downs:
+            down.taken().start()
+        all_greet(me)
+        for one in loads:
+            one.wait()
+        for group in groups:
+            group.start(0)
+
+        @pl.loop(0, TOKENS // 128)
+        def _(i):
+            rows = pl.ds(pl.multiple_of(i * 128, 128), 128)
+            wide = x_ref[rows, :].astype(F32)
+            scale = lax.rsqrt(jnp.mean(wide**2, -1, keepdims=True) + 1e-6)
+            for k in range(4):
+                there, _ = me.along("x", k)
+                cols = pl.ds(pl.multiple_of(there * (D // 4), D // 4), D // 4)
+                a[rows, pl.ds(k * (D // 4), D // 4)] = (x_ref[rows, cols].astype(F32) * scale).astype(BF)
+
+        onward(groups[0], 0)
+        onward(groups[1], 0)
+        onward(groups[0], 1)
+        onward(groups[2], 0)
+        groups[0].finish(2)
+        for down in downs:
+            down.taken().wait()
+            down.put().start()
+
+    def part(rows_of):
+        for rows in rows_of:
+            both = dot(a[rows, :], w[j].reshape(D, 2 * TN))
+            gate, up = both[:, :TN], both[:, TN:]
+            sig = jax.nn.sigmoid(gate)
+            silu = gate * sig
+            by_up_ref[rows, :] = silu
+            by_gate_ref[rows, :] = up * (sig + silu * (1.0 - sig))
+            hid_ref[rows, :] = (silu * up).astype(BF)
+
+    rows_of = split_rows(TOKENS, 256)
+    part(rows_of[:4])
+
+    @pl.when(j == 0)
+    def _():
+        onward(groups[1], 1)
+        onward(groups[3], 0)
+        downs[0].start(0)
+
+    @pl.when(j == 1)
+    def _():
+        onward(groups[2], 1)
+        onward(groups[4], 0)
+        downs[1].start(0)
+
+    @pl.when(j == 2)
+    def _():
+        onward(groups[3], 1)
+
+    @pl.when(j == 4)
+    def _():
+        onward(groups[4], 1)
+        onward(downs[1], 0)
+
+    part(rows_of[4:])
+
+    @pl.when(j == 0)
+    def _():
+        groups[1].finish(2)
+
+    @pl.when(j == 1)
+    def _():
+        groups[2].finish(2)
+
+    @pl.when(j == 2)
+    def _():
+        groups[3].finish(2)
+
+    @pl.when(j == 3)
+    def _():
+        onward(downs[0], 0)
+
+    @pl.when(j == 4)
+    def _():
+        groups[4].finish(2)
+
+    @pl.when(j == 6)
+    def _():
+        for down in downs:
+            onward(down, 1)
+        for down in downs:
+            down.finish(2)
+            down.put().wait()
+
+
+def first_layer_forward(x, wg, wu, wd):
+    tile = pl.BlockSpec((TOKENS, TN), lambda j: (0, j))
+    anywhere = pl.BlockSpec(memory_space=pl.ANY)
+    full = jax.ShapeDtypeStruct((4, 2, FF // 8, D), BF)
+    dma = pltpu.SemaphoreType.DMA
+    hid, by_gate, by_up, wd0, wd1 = pl.pallas_call(
+        first_layer_forward_kernel,
+        grid=(FF // TN,),
+        in_specs=[pl.BlockSpec((TOKENS, D), lambda j: (0, 0), pipeline_mode=pl.Buffered(1)), anywhere, anywhere, anywhere],
+        out_specs=[tile, tile, tile, anywhere, anywhere],
+        out_shape=[jax.ShapeDtypeStruct((TOKENS, FF), t) for t in (BF, F32, F32)] + [full, full],
+        scratch_shapes=[
+            pltpu.VMEM((FF // TN, 4, 2, D // 8, 2 * TN), BF),
+            pltpu.VMEM((TOKENS, D), BF),
+            pltpu.VMEM((FF // 8, D), BF),
+            pltpu.VMEM((FF // 8, D), BF),
+            dma((FF // TN, 2)),
+            dma((len(GROUPS), 3, 2, 3)),
+            dma((len(GROUPS), 3, 2, 3)),
+            *[dma((3, 18)), dma((3, 18)), dma((2,))] * 2,
+        ],
+        compiler_params=pltpu.CompilerParams(vmem_limit_bytes=60 * MIB, collective_id=1, has_side_effects=True),
+        cost_estimate=cost(4 * TOKENS * D * FF, 100 * MIB),
+        name="first_layer_forward",
+    )(x, wg, wu, wd)
+    return hid, by_gate, by_up, wd0.reshape(FF, D), wd1.reshape(FF, D)
 
 
 class Summed:
@@ -460,25 +663,23 @@
     def step(x, dy, *arrays):
         weights, m, v = (arrays[i : i + 3] for i in (0, 3, 6))
         x, dy = x[0], dy[0]
-        place = lax.axis_index("r")
-        rows = weights[0].shape[1] // 16
-        mine = [lax.dynamic_slice_in_dim(weights[n][layer], place * rows, rows, 0) for layer in (0, 1) for n in (0, 1)]
-        w = lax.all_gather(jnp.concatenate(mine, 1), ("s", "r"), axis=0, tiled=True)
-        wd = [lax.all_gather(weights[2][layer], "s", axis=0, tiled=True) for layer in (0, 1)]
-
-        a0 = normed(x)
-        hid0, gate0, up0 = gate_up(a0, w, 0)
-        h1 = x + dot(hid0, wd[0]).astype(BF)
+        place, rows = lax.axis_index("r"), weights[0].shape[1] // 16
+        mine = [lax.dynamic_slice(w, (1, place * rows, 0), (1, rows, FF))[0] for w in weights[:2]]
+        w1 = lax.all_gather(jnp.concatenate(mine, 1), ("s", "r"), axis=0, tiled=True)
+
+        hid0, by_gate0, by_up0, wd0, wd1 = first_layer_forward(x, *weights)
+        h1 = x + dot(hid0, wd0).astype(BF)
         a1 = normed(h1)
-        hid1, dg1, du1 = last_layer(a1, dy, w, 2, wd[1])
+        hid1, dg1, du1 = last_layer(a1, dy, w1, wd1)
 
         def scattered(term):
             return lax.psum_scatter(term, "s", scatter_dimension=0, tiled=True)
 
         terms = [scattered(dot(a, b, TNN).astype(BF)) for a, b in ((hid1, dy), (a1, dg1), (a1, du1))]
-        dh1 = norm_grad(dg1, du1, w, 2, h1, dy)
+        dh1 = norm_grad(dg1, du1, w1, h1, dy)
         down0 = dot(hid0, dh1, TNN).astype(BF)
-        dg0, du0 = act_grad(dh1, wd[0], gate0, up0)
+        dg0, du0 = act_grad(dh1, wd0, by_gate0, by_up0)
+        a0 = normed(x)
         d1, g1, u1 = (lax.psum(t, "r") for t in terms)
         g0, u0, d0 = first_layer_grads(a0, dg0, du0, down0)
         gradients = [jnp.stack(pair).astype(F32) for pair in ((g0, g1), (u0, u1), (d0, d1))]

time: 634 us -> 558 us (0.88)
  waiting for transfers between devices: 107 us -> 0.11 us
  Pallas kernels: 352 us -> 391 us
  local copies, waits for them, and re-layouts: 14.6 us -> 6.97 us
    all_gather x3 -> x1, waiting for transfers between devices: 106 us -> 0.01 us  [step(): lax.all_gather(jnp.concatenate(mine, 1), ('s', 'r'), axis=0, tiled=True)]
    pallas_call x3, Pallas kernels: 162 us -> 201 us  [the longest x1 105 us: first_layer_forward(): pl.pallas_call(first_layer_forward_kernel, grid=(FF // TN,), in_specs=[pl...]
    slice x3 -> x0, local copies, waits for them, and re-layouts: 6.79 us -> none  [the longest x2 3.96 us: step(): weights[n][layer]]
  transfers between devices with their start and end apart: 7 -> 5, of which waited for: 2 -> 0; matrix products, arithmetic and copies ran while one was open for 16% -> 17% of each run, Pallas kernels for 47% -> 61%
where the time goes in v2:
time: 558 us; the launch traced here: 550 us
  Pallas kernels  391 us (70%)
  matrix products  110 us (20%)
  other arithmetic  27.8 us (5%)
  between operations  14.4 us (3%)
  local copies, waits for them, and re-layouts  6.97 us (1%)
    pallas_call x1, Pallas kernels, first_layer_grads(): pl.pallas_call(first_layer_kernel, grid=(2 * steps,), in_specs=[pl.BlockS...  142 us
    dot_general x5, matrix products, dot(): return lax.dot_general(a, b, dims, preferred_element_type=F32)  110 us
    pallas_call x1, Pallas kernels, first_layer_forward(): pl.pallas_call(first_layer_forward_kernel, grid=(FF // TN,), in_specs=[pl...  105 us
    pallas_call x1, Pallas kernels, last_layer(): pl.pallas_call(last_layer_kernel, grid=(FF // tn,), in_specs=[wide, wide,...  57 us
    pallas_call x1, Pallas kernels, norm_grad(): pl.pallas_call(norm_grad_kernel, grid=(TOKENS // tm, FF // TN), in_specs=...  48.3 us
    pallas_call x1, Pallas kernels, act_grad(): pl.pallas_call(act_grad_kernel, grid=(FF // TN,), in_specs=[pl.BlockSpec(...  39.3 us
    convert_element_type x3, other arithmetic, adamw(): return ((w - 0.02 * step).astype(BF), m, v)  18.4 us
  transfers between devices with their start and end apart: 5, of which 0 were waited for; matrix products, arithmetic and copies ran while one was open for 17% of the time, Pallas kernels for 61%

profile of v2, /device:TPU:0, one launch (start us, length us, event | category | flops | bytes accessed | tf_op | source)
XLA Modules:
  0.0 550.3 jit_solution(11478749909334131372)
XLA Ops:
  7.2 0.9 dynamic-slice_bitcast_fusion
  8.1 0.7 pad_maximum_fusion.3
  8.8 104.8 %first_layer_forward.1 = (bf16[2048,3584]{1,0:T(8,128)(2,1)}, f32[2048,3584]{1,0:T(8,128)}, f32[2048,3584]{1,0:T(8,128)}, bf16[4,2,448,1024]{3,2,1,0:T(8,128)(2,1)}, bf16[4,2,448,1024]{3,2,1,0:T(8,128)(2,1)}) custom-call(bf16[2048,1024]{1,0:T(8,128)(2,1)} %bitcast.29, bf16[2,128,3584]{2,1,0:T(8,128)(2,1)} %wg_ref.1, bf16[2,128,3584]{2,1,0:T(8,128)(2,1)} %wu_ref.1, ...), custom_call_target="tpu_custom_call" | custom-call | flops 30064771072 | bytes 104857600 | tf_op jit(solution)/shard_map/first_layer_forward/pallas_call | solution.py:398
  113.6 20.9 %fusion.2 = (f32[2048]{0:T(1024)S(1)}, bf16[2048,1024]{1,0:T(8,128)(2,1)S(1)}) fusion(bf16[2048,3584]{1,0:T(8,128)(2,1)} %get-tuple-element.22, bf16[3584,1024]{1,0:T(8,128)(2,1)} %bitcast.30, bf16[1,2048,1024]{2,1,0:T(8,128)(2,1)} %param.11), kind=kOutput, calls=%fused_computation.6 | convolution fusion | flops 15042869248 | bytes 30416896 | tf_op jit(solution)/shard_map/dot_general | solution.py:22
  134.5 2.0 copy-done.1
  136.6 2.8 fusion.3.a_ref
  139.3 57.0 %last_layer.1 = (bf16[2048,3584]{1,0:T(8,128)(2,1)}, bf16[2048,3584]{1,0:T(8,128)(2,1)}, bf16[2048,3584]{1,0:T(8,128)(2,1)}) custom-call(bf16[2048,1024]{1,0:T(8,128)(2,1)} %fusion.3.a_ref, bf16[2048,1024]{1,0:T(8,128)(2,1)} %bitcast.38, bf16[1024,7168]{1,0:T(8,128)(2,1)} %all-gather.2.cloned.1.call-done.wg_ref.wu_ref, ...), custom_call_target="tpu_custom_call" | custom-call | flops 45097156608 | bytes 83886080 | tf_op jit(solution)/shard_map/last_layer/pallas_call | solution.py:71
  196.3 22.1 %convolution_convert_fusion.1 = bf16[1024,3584]{1,0:T(8,128)(2,1)} fusion(bf16[2048,1024]{1,0:T(8,128)(2,1)} %fusion.3.a_ref, bf16[2048,3584]{1,0:T(8,128)(2,1)} %get-tuple-element.26.du_ref), kind=kOutput, calls=%fused_computation.9 | convolution fusion | flops 15036055552 | bytes 26214400 | tf_op jit(solution)/shard_map/dot_general | solution.py:22
  218.5 22.5 %convolution_convert_fusion.2 = bf16[1024,3584]{1,0:T(8,128)(2,1)} fusion(bf16[2048,1024]{1,0:T(8,128)(2,1)} %fusion.3.a_ref, bf16[2048,3584]{1,0:T(8,128)(2,1)} %get-tuple-element.25.dg_ref), kind=kOutput, calls=%fused_computation.10 | convolution fusion | flops 15036055552 | bytes 26214400 | tf_op jit(solution)/shard_map/dot_general | solution.py:22
  241.1 22.1 %convolution_convert_fusion = bf16[3584,1024]{1,0:T(8,128)(2,1)} fusion(bf16[2048,3584]{1,0:T(8,128)(2,1)} %get-tuple-element.34, bf16[1,2048,1024]{2,1,0:T(8,128)(2,1)} %param.12), kind=kOutput, calls=%fused_computation.8 | convolution fusion | flops 15036055552 | bytes 26214400 | tf_op jit(solution)/shard_map/dot_general | solution.py:22
  263.3 3.2 fusion
  266.8 2.7 fusion.1.a_ref
  269.5 48.3 %norm_grad.1.dh_ref = bf16[2048,1024]{1,0:T(8,128)(2,1)} custom-call(bf16[2048,3584]{1,0:T(8,128)(2,1)} %get-tuple-element.25.dg_ref, bf16[2048,3584]{1,0:T(8,128)(2,1)} %get-tuple-element.26.du_ref, bf16[1024,7168]{1,0:T(8,128)(2,1)} %all-gather.2.cloned.1.call-done.wg_ref.wu_ref, bf16[1024,7168]{1,0:T(8,128)(2,1)} %all-gather.2.cloned.1.call-done.wg_ref.wu_ref, ...), custom_call_target="tpu_custom_call" | custom-call | flops 30064771072 | bytes 62914560 | tf_op jit(solution)/shard_map/norm_grad/pallas_call | solution.py:144
  317.8 39.3 %act_grad.1 = (bf16[2048,3584]{1,0:T(8,128)(2,1)}, bf16[2048,3584]{1,0:T(8,128)(2,1)}) custom-call(bf16[2048,1024]{1,0:T(8,128)(2,1)} %norm_grad.1.dh_ref, bf16[3584,1024]{1,0:T(8,128)(2,1)} %bitcast.31, f32[2048,3584]{1,0:T(8,128)} %get-tuple-element.27.by_gate_ref, f32[2048,3584]{1,0:T(8,128)} %get-tuple-element.28.by_up_ref), custom_call_target="tpu_custom_call" | custom-call | flops 15032385536 | bytes 125829120 | tf_op jit(solution)/shard_map/act_grad/pallas_call | solution.py:98
  357.2 22.0 %convolution_convert_fusion.3 = bf16[3584,1024]{1,0:T(8,128)(2,1)} fusion(bf16[2048,3584]{1,0:T(8,128)(2,1)} %get-tuple-element.22, bf16[2048,1024]{1,0:T(8,128)(2,1)} %norm_grad.1.dh_ref), kind=kOutput, calls=%fused_computation.11 | convolution fusion | flops 15036055552 | bytes 26214400 | tf_op jit(solution)/shard_map/dot_general | solution.py:22
  379.2 141.8 %first_layer_grads.1 = (bf16[448,1024]{1,0:T(8,128)(2,1)}, bf16[128,3584]{1,0:T(8,128)(2,1)}, bf16[128,3584]{1,0:T(8,128)(2,1)}) custom-call(bf16[2048,1024]{1,0:T(8,128)(2,1)} %fusion.1.a_ref, bf16[2048,3584]{1,0:T(8,128)(2,1)} %get-tuple-element.29.dg_ref, bf16[2048,3584]{1,0:T(8,128)(2,1)} %get-tuple-element.30.du_ref, bf16[4,2,448,1024]{3,2,1,0:T(8,128)(2,1)} %bitcast.40), custom_call_target="tpu_custom_call" | custom-call | flops 30064771072 | bytes 62914560 | tf_op jit(solution)/shard_map/first_layer_grads/pallas_call | solution.py:624
  521.1 8.4 %fusion.14 = (bf16[2,448,1024]{2,1,0:T(8,128)(2,1)}, f32[2,448,1024]{2,1,0:T(8,128)}, f32[2,448,1024]{2,1,0:T(8,128)}) fusion(bf16[2,448,1024]{2,1,0:T(8,128)(2,1)} %wd_ref.1, bf16[1,448,1024]{2,1,0:T(8,128)(2,1)} %get-tuple-element.37, bf16[1,448,1024]{2,1,0:T(8,128)(2,1)} %bitcast.37, f32[2,448,1024]{2,1,0:T(8,128)} %param.21, f32[2,448,1024]{2,1,0:T(8,128)} %param.18), kind=kLoop, calls=%fused_computation.35 | loop fusion | flops 17432576 | bytes 20185088 | tf_op jit(solution)/shard_map/convert_element_type | solution.py:43
  529.4 1.1 copy-done.3
  530.6 0.5 copy-done.6
  531.2 0.3 copy-done.11
  531.5 5.5 %fusion.10 = (bf16[2,128,3584]{2,1,0:T(8,128)(2,1)}, f32[2,128,3584]{2,1,0:T(8,128)}, f32[2,128,3584]{2,1,0:T(8,128)}) fusion(bf16[2,128,3584]{2,1,0:T(8,128)(2,1)S(1)} %copy-done.6, bf16[1,128,3584]{2,1,0:T(8,128)(2,1)S(1)} %copy-done.9, bf16[1,128,3584]{2,1,0:T(8,128)(2,1)S(1)} %bitcast.36, f32[2,128,3584]{2,1,0:T(8,128)S(1)} %copy-done.2, ...), kind=kLoop, calls=%fused_computation.31 | loop fusion | flops 17432576 | bytes 20185088 | tf_op jit(solution)/shard_map/convert_element_type | solution.py:43
  537.1 0.3 copy-done.5
  537.3 1.0 copy-done.7
  538.8 4.5 fusion.6
  (35 shorter events, 1.2 us)
Async XLA Ops:
  7.2 132.1 %all-gather.2.cloned.1.call-start = ((), (), s32[]{:S(2)}) async-start(), calls=%async_computation.3 | async-start | bytes 14794752 | tf_op jit(solution)/shard_map/all_gather | solution.py:668
  8.8 370.4 %reduce-scatter.6.cloned.1.call-start = ((), (), s32[]{:S(2)}) async-start(), calls=%async_computation.5 | async-start | bytes 8257536 | tf_op jit(solution)/shard_map/reduce_scatter | solution.py:676
  134.5 2.1 copy-start.1
  218.5 160.7 %reduce-scatter.4.cloned.1.call-start = ((), (), s32[]{:S(2)}) async-start(), calls=%async_computation.4 | async-start | bytes 8257536 | tf_op jit(solution)/shard_map/reduce_scatter | solution.py:676
  241.0 138.1 %reduce-scatter.8.cloned.1.call-start = ((), (), s32[]{:S(2)}) async-start(), calls=%async_computation.6 | async-start | bytes 8257536 | tf_op jit(solution)/shard_map/reduce_scatter | solution.py:676
  263.3 257.7 %all-reduce.3.cloned.1.call-start = ((), (), s32[]{:S(2)}) async-start(), calls=%async_computation.7 | async-start | bytes 5505024 | tf_op jit(solution)/shard_map/psum | solution.py:683
  263.3 3.5 copy-start
  521.0 8.4 %copy-start.2 = (f32[2,128,3584]{2,1,0:T(8,128)S(1)}, f32[2,128,3584]{2,1,0:T(8,128)}, u32[]{:S(2)}) copy-start(f32[2,128,3584]{2,1,0:T(8,128)} %param.20) | copy-start | bytes 11010052
  521.0 9.5 %copy-start.3 = (f32[2,128,3584]{2,1,0:T(8,128)S(1)}, f32[2,128,3584]{2,1,0:T(8,128)}, u32[]{:S(2)}) copy-start(f32[2,128,3584]{2,1,0:T(8,128)} %param.17) | copy-start | bytes 11010052
  521.0 10.0 %copy-start.6 = (bf16[2,128,3584]{2,1,0:T(8,128)(2,1)S(1)}, bf16[2,128,3584]{2,1,0:T(8,128)(2,1)}, u32[]{:S(2)}) copy-start(bf16[2,128,3584]{2,1,0:T(8,128)(2,1)} %wu_ref.1) | copy-start | bytes 5505028
  521.0 10.2 %copy-start.9 = (bf16[1,128,3584]{2,1,0:T(8,128)(2,1)S(1)}, bf16[1,128,3584]{2,1,0:T(8,128)(2,1)}, u32[]{:S(2)}) copy-start(bf16[1,128,3584]{2,1,0:T(8,128)(2,1)} %get-tuple-element.36) | copy-start | bytes 2752516
  521.0 10.5 %copy-start.11 = (bf16[128,3584]{1,0:T(8,128)(2,1)S(1)}, bf16[128,3584]{1,0:T(8,128)(2,1)}, u32[]{:S(2)}) copy-start(bf16[128,3584]{1,0:T(8,128)(2,1)} %get-tuple-element.32) | copy-start | bytes 2752516
  531.5 5.5 %copy-start.4 = (f32[2,128,3584]{2,1,0:T(8,128)S(1)}, f32[2,128,3584]{2,1,0:T(8,128)}, u32[]{:S(2)}) copy-start(f32[2,128,3584]{2,1,0:T(8,128)} %param.19) | copy-start | bytes 11010052
  531.5 5.8 %copy-start.5 = (f32[2,128,3584]{2,1,0:T(8,128)S(1)}, f32[2,128,3584]{2,1,0:T(8,128)}, u32[]{:S(2)}) copy-start(f32[2,128,3584]{2,1,0:T(8,128)} %param.16) | copy-start | bytes 11010052
  531.5 6.8 %copy-start.7 = (bf16[2,128,3584]{2,1,0:T(8,128)(2,1)S(1)}, bf16[2,128,3584]{2,1,0:T(8,128)(2,1)}, u32[]{:S(2)}) copy-start(bf16[2,128,3584]{2,1,0:T(8,128)(2,1)} %wg_ref.1) | copy-start | bytes 5505028
  531.5 7.0 %copy-start.8 = (bf16[1,128,3584]{2,1,0:T(8,128)(2,1)S(1)}, bf16[1,128,3584]{2,1,0:T(8,128)(2,1)}, u32[]{:S(2)}) copy-start(bf16[1,128,3584]{2,1,0:T(8,128)(2,1)} %get-tuple-element.35) | copy-start | bytes 2752516
  531.5 7.3 %copy-start.10 = (bf16[128,3584]{1,0:T(8,128)(2,1)S(1)}, bf16[128,3584]{1,0:T(8,128)(2,1)}, u32[]{:S(2)}) copy-start(bf16[128,3584]{1,0:T(8,128)(2,1)} %get-tuple-element.31) | copy-start | bytes 2752516
Sparse Core Ops, SparseCore 0:
  11.5 103.7 all-gather.1
  218.6 47.3 reduce-scatter.5
  268.5 47.1 reduce-scatter.3
  317.9 47.1 reduce-scatter.7
  379.3 134.1 all-reduce.2

commit v3 on v0

v3 whole, which is shorter than its diff:
```python
import jax
import jax.numpy as jnp
from jax import lax
from jax.experimental import pallas as pl
from jax.experimental.pallas import tpu as pltpu
from jax.sharding import PartitionSpec as P

BF, F32 = jnp.bfloat16, jnp.float32
MIB = 1 << 20
TOKENS, D, FF = 2048, 1024, 3584
TN = 512
MESH = pl.DeviceIdType.MESH

NN = (((1,), (0,)), ((), ()))
NT = (((1,), (1,)), ((), ()))
TNN = (((0,), (0,)), ((), ()))


def dot(a, b, dims=NN):
    return lax.dot_general(a, b, dims, preferred_element_type=F32)


def params(**kw):
    return pltpu.CompilerParams(vmem_limit_bytes=60 * MIB, **kw)


def cost(flops, nbytes):
    return pl.CostEstimate(flops=flops, bytes_accessed=nbytes, transcendentals=0)


def normed(h):
    wide = h.astype(F32)
    scale = lax.rsqrt(jnp.mean(wide**2, -1, keepdims=True) + 1e-6)
    return (wide * scale).astype(BF)


def adamw(w, m, v, g):
    m = 0.9 * m + 0.1 * g
    v = 0.95 * v + 0.05 * g * g
    step = m * lax.rsqrt(v + 1e-8) + 0.1 * w
    return (w - 0.02 * step).astype(BF), m, v


def split_rows(rows, chunk):
    return [pl.ds(i * chunk, chunk) for i in range(rows // chunk)]


def grads_of_act(gate, up, d_hidden):
    sig = jax.nn.sigmoid(gate)
    silu = gate * sig
    d = d_hidden.astype(BF).astype(F32)
    return silu * up, d * up * (sig + silu * (1.0 - sig)), d * silu


def last_layer_kernel(a_ref, dy_ref, wg_ref, wu_ref, wd_ref, hid_ref, dg_ref, du_ref):
    for rows in split_rows(a_ref.shape[0], 256):
        a = a_ref[rows, :]
        gate, up = dot(a, wg_ref[...]), dot(a, wu_ref[...])
        hid, dg, du = grads_of_act(gate, up, dot(dy_ref[rows, :], wd_ref[...], NT))
        hid_ref[rows, :] = hid.astype(BF)
        dg_ref[rows, :] = dg.astype(BF)
        du_ref[rows, :] = du.astype(BF)


def last_layer(a, dy, w, wd):
    tn = 256
    tile = pl.BlockSpec((TOKENS, tn), lambda j: (0, j))
    wide = pl.BlockSpec((TOKENS, D), lambda j: (0, 0), pipeline_mode=pl.Buffered(1))
    return pl.pallas_call(
        last_layer_kernel,
        grid=(FF // tn,),
        in_specs=[
            wide,
            wide,
            pl.BlockSpec((D, tn), lambda j: (0, j)),
            pl.BlockSpec((D, tn), lambda j: (0, FF // tn + j)),
            pl.BlockSpec((tn, D), lambda j: (j, 0)),
        ],
        out_specs=[tile, tile, tile],
        out_shape=[jax.ShapeDtypeStruct((TOKENS, FF), BF)] * 3,
        compiler_params=params(),
        cost_estimate=cost(6 * TOKENS * D * FF, 80 * MIB),
        name="last_layer",
    )(a, dy, w, w, wd)


class Place:
    def __init__(self):
        r, s = lax.axis_index("r"), lax.axis_index("s")
        self.r, self.s = r, s
        self.y, self.z = lax.div(r, 4), lax.rem(r, 4)
        self.x, self.c = lax.div(s, 2), lax.rem(s, 2)

    def partner(self):
        return (0, self.r, self.x * 2 + 1 - self.c)

    def along(self, axis, k):
        here = getattr(self, axis)
        there = lax.rem(here + k, 4)
        at = {"x": self.x, "y": self.y, "z": self.z, axis: there}
        return there, (0, at["y"] * 4 + at["z"], at["x"] * 2 + self.c)


def all_greet(me):
    barrier = pltpu.get_barrier_semaphore()
    peers = [me.partner()] + [me.along(axis, k)[1] for axis in "xyz" for k in (1, 2, 3)]
    for peer in peers:
        pl.semaphore_signal(barrier, inc=1, device_id=peer, device_id_type=MESH)
    pl.semaphore_wait(barrier, len(peers))


GROUPS = ((0, 1), (1, 1), (2, 1), (3, 2), (5, 2))


class Gathered:
    def __init__(self, me, w, number, sems):
        self.me, self.number, self.stage = me, number, -1
        self.send, self.recv = sems
        first, count = GROUPS[number]
        self.w = w.at[pl.ds(first, count)]

    def rows(self, color):
        quarter = D // 64
        where = self.me.y if color == 0 else self.me.z
        return pl.ds(pl.multiple_of((color * 4 + where) * quarter, quarter), quarter)

    def copies(self, stage):
        me, w, made = self.me, self.w, []

        def copy(src, dst, color, k, device):
            at = (self.number, stage, color, k)
            made.append(pltpu.make_async_remote_copy(src_ref=src, dst_ref=dst, send_sem=self.send.at[at], recv_sem=self.recv.at[at], device_id=device, device_id_type=MESH))

        if stage == 2:
            copy(w.at[:, :, me.c], w.at[:, :, me.c], 0, 0, me.partner())
            return made
        for color in (0, 1):
            rows = self.rows(color)
            for k in (1, 2, 3):
                if stage == 0:
                    copy(w.at[:, 0, me.c, rows], w.at[:, 4 - k, me.c, rows], color, k - 1, me.along("x", k)[1])
                else:
                    others = w.at[:, pl.ds(1, 3), me.c, rows]
                    copy(others, others, color, k - 1, me.along("yz"[color], k)[1])
        return made

    def advance(self):
        if self.stage >= 0:
            for one in self.copies(self.stage):
                one.wait()
        self.stage += 1
        if self.stage < 3:
            for one in self.copies(self.stage):
                one.start()


class GatheredDown:
    def __init__(self, me, own, out, held, sems):
        self.me, self.own, self.out, self.held, self.stage = me, own, out, held, -1
        self.send, self.recv, self.local = sems
        self.part, self.half = own.shape[0] // 4, own.shape[1] // 2

    def piece(self, color):
        where = self.me.y if color == 0 else self.me.z
        return pl.ds(pl.multiple_of(where * self.part, self.part), self.part), pl.ds(color * self.half, self.half)

    def copies(self, stage):
        me, out, made = self.me, self.out, []

        def copy(src, dst, n, device):
            at = (stage, n)
            made.append(pltpu.make_async_remote_copy(src_ref=src, dst_ref=dst, send_sem=self.send.at[at], recv_sem=self.recv.at[at], device_id=device, device_id_type=MESH))

        if stage == 2:
            copy(self.own, out.at[me.x, me.c], 0, me.partner())
            for k in (1, 2, 3):
                x, _ = me.along("x", k)
                copy(out.at[x, me.c], out.at[x, me.c], k, me.partner())
            return made
        for color in (0, 1):
            rows, cols = self.piece(color)
            for k in (1, 2, 3):
                if stage == 0:
                    copy(self.own.at[rows, cols], out.at[me.x, me.c, rows, cols], color * 3 + k - 1, me.along("x", k)[1])
                    continue
                for other in (1, 2, 3):
                    there = out.at[me.along("x", other)[0], me.c, rows, cols]
                    copy(there, there, (color * 3 + k - 1) * 3 + other - 1, me.along("yz"[color], k)[1])
        return made

    def taken(self):
        return pltpu.make_async_copy(self.own, self.held, self.local.at[0])

    def put(self):
        return pltpu.make_async_copy(self.held, self.out.at[self.me.x, self.me.c], self.local.at[1])

    def advance(self):
        if self.stage >= 0:
            for one in self.copies(self.stage):
                one.wait()
        self.stage += 1
        if self.stage < 3:
            for one in self.copies(self.stage):
                one.start()


FORWARD_STEPS = (("bdm", "b"), ("cen", "c"), ("d", "d"), ("", "m"), ("en", "e"), ("", ""), ("", "mnmn"))
FORWARD_MIDWAY, FORWARD_AFTER = zip(*FORWARD_STEPS, strict=True)


def first_layer_forward_kernel(x_ref, wg_ref, wu_ref, wd_ref, hid_ref, by_gate_ref, by_up_ref, wd0_ref, wd1_ref, a0_ref, w, a, held0, held1, load, out, *sems):
    j = pl.program_id(0)
    me = Place()
    groups = [Gathered(me, w, n, sems[:2]) for n in range(len(GROUPS))]
    downs = [GatheredDown(me, wd_ref.at[n], out, held, sems[2 + 3 * n : 5 + 3 * n]) for n, (out, held) in enumerate(((wd0_ref, held0), (wd1_ref, held1)))]
    named = dict(zip("abcdemn", groups + downs, strict=True))
    loads = []
    for chunk in range(FF // TN):
        for n, ref in enumerate((wg_ref, wu_ref)):
            src = ref.at[0, :, pl.ds(chunk * TN, TN)]
            loads.append(pltpu.make_async_copy(src, w.at[chunk, 0, me.c, :, pl.ds(n * TN, TN)], load.at[chunk, n]))

    saves = []
    for k in range(4):
        cols = pl.ds(pl.multiple_of(me.along("x", k)[0] * (D // 4), D // 4), D // 4)
        saves.append(pltpu.make_async_copy(a.at[:, pl.ds(k * (D // 4), D // 4)], a0_ref.at[:, cols], out.at[k]))

    @pl.when(j == 0)
    def _():
        for one in loads:
            one.start()
        for down in downs:
            down.taken().start()
        all_greet(me)
        for one in loads:
            one.wait()
        for group in groups:
            group.advance()

        @pl.loop(0, TOKENS // 128)
        def _(i):
            rows = pl.ds(pl.multiple_of(i * 128, 128), 128)
            wide = x_ref[rows, :].astype(F32)
            scale = lax.rsqrt(jnp.mean(wide**2, -1, keepdims=True) + 1e-6)
            for k in range(4):
                there, _ = me.along("x", k)
                cols = pl.ds(pl.multiple_of(there * (D // 4), D // 4), D // 4)
                a[rows, pl.ds(k * (D // 4), D // 4)] = (x_ref[rows, cols].astype(F32) * scale).astype(BF)

        for name in "abaca":
            named[name].advance()
        for down in downs:
            down.taken().wait()
            down.put().start()
        for one in saves:
            one.start()

    def part(rows_of):
        for rows in rows_of:
            both = dot(a[rows, :], w[j].reshape(D, 2 * TN))
            gate, up = both[:, :TN], both[:, TN:]
            sig = jax.nn.sigmoid(gate)
            silu = gate * sig
            by_up_ref[rows, :] = silu
            by_gate_ref[rows, :] = up * (sig + silu * (1.0 - sig))
            hid_ref[rows, :] = (silu * up).astype(BF)

    rows_of = split_rows(TOKENS, 256)
    part(rows_of[: len(rows_of) // 2])
    run_schedule(j, FORWARD_MIDWAY, named)
    part(rows_of[len(rows_of) // 2 :])
    run_schedule(j, FORWARD_AFTER, named)

    @pl.when(j == pl.num_programs(0) - 1)
    def _():
        for one in saves + [down.put() for down in downs]:
            one.wait()


def first_layer_forward(x, wg, wu, wd):
    tile = pl.BlockSpec((TOKENS, TN), lambda j: (0, j))
    anywhere = pl.BlockSpec(memory_space=pl.ANY)
    full = jax.ShapeDtypeStruct((4, 2, FF // 8, D), BF)
    dma = pltpu.SemaphoreType.DMA
    hid, by_gate, by_up, wd0, wd1, a0 = pl.pallas_call(
        first_layer_forward_kernel,
        grid=(FF // TN,),
        in_specs=[pl.BlockSpec((TOKENS, D), lambda j: (0, 0), pipeline_mode=pl.Buffered(1)), anywhere, anywhere, anywhere],
        out_specs=[tile, tile, tile, anywhere, anywhere, anywhere],
        out_shape=[jax.ShapeDtypeStruct((TOKENS, FF), t) for t in (BF, F32, F32)] + [full, full, jax.ShapeDtypeStruct((TOKENS, D), BF)],
        scratch_shapes=[
            pltpu.VMEM((FF // TN, 4, 2, D // 8, 2 * TN), BF),
            pltpu.VMEM((TOKENS, D), BF),
            pltpu.VMEM((FF // 8, D), BF),
            pltpu.VMEM((FF // 8, D), BF),
            dma((FF // TN, 2)),
            dma((4,)),
            dma((len(GROUPS), 3, 2, 3)),
            dma((len(GROUPS), 3, 2, 3)),
            *[dma((3, 18)), dma((3, 18)), dma((2,))] * 2,
        ],
        compiler_params=pltpu.CompilerParams(vmem_limit_bytes=60 * MIB, collective_id=1, has_side_effects=True),
        cost_estimate=cost(4 * TOKENS * D * FF, 100 * MIB),
        name="first_layer_forward",
    )(x, wg, wu, wd)
    return hid, by_gate, by_up, wd0.reshape(FF, D), wd1.reshape(FF, D), a0


SUM_GROUPS = ((0, 2), (2, 2), (4, 2), (6, 1))
STAGES = 5


class Summed:
    def __init__(self, me, term, core, away, buffers, sems, at, place):
        self.me, self.term, self.core, self.away, self.place, self.at = me, term, core, away, place, at
        self.from_core, self.first, self.second, self.third = buffers
        self.send, self.recv, self.local = sems
        self.count, self.part = term.shape[0], term.shape[-2] // 4
        self.stage = -1

    def rows(self, where):
        return pl.ds(pl.multiple_of(where * self.part, self.part), self.part)

    def axes(self, color):
        main, other = ("y", "z") if color == 0 else ("z", "y")
        return main, other, self.rows(getattr(self.me, main))

    def copies(self, stage):
        me, term, core, made = self.me, self.term, self.core, []

        def copy(src, dst, color, k, device):
            at = (*self.at, stage, color, k)
            made.append(pltpu.make_async_remote_copy(src_ref=src, dst_ref=dst, send_sem=self.send.at[at], recv_sem=self.recv.at[at], device_id=device, device_id_type=MESH))

        if stage == 0:
            for n, (src, dst) in enumerate(self.away):
                copy(src, dst, n, 0, me.partner())
            return made
        for color in range(2):
            main, other, mine = self.axes(color)
            for k in range(3):
                there, device = me.along({2: "x", 3: other}.get(stage, main), k + 1)
                if stage == 1:
                    copy(term.at[:, color, :, core, self.rows(there)], self.first.at[:, color, k], color, k, device)
                elif stage == 2:
                    copy(term.at[:, color, there, core, mine], self.second.at[:, color, k], color, k, device)
                elif stage == 3:
                    copy(term.at[:, color, me.x, core, mine], self.third.at[:, color, getattr(me, other)], color, k, device)
                else:
                    for n, (src, dst) in enumerate(self.outward(color)):
                        copy(src, dst, color, 3 * n + k, device)
        return made

    def outward(self, color):
        rows = self.axes(color)[-1]
        return [(self.term.at[n, color, self.me.x, self.core, rows], self.place(n, color, rows)) for n in range(self.count)]

    def kept(self):
        return [pltpu.make_async_copy(src, dst, self.local.at[(*self.at, color, n)]) for color in range(2) for n, (src, dst) in enumerate(self.outward(color))]

    def advance(self):
        assert self.stage < STAGES
        if self.stage >= 0:
            self.finish(self.stage)
        self.stage += 1
        if self.stage < STAGES:
            self.start(self.stage)

    def start(self, stage):
        me = self.me
        if stage == 3:
            for color in range(2):
                _, other, rows = self.axes(color)
                self.third[:, color, getattr(me, other)] = self.term[:, color, me.x, self.core, rows]
        for one in self.copies(stage):
            one.start()
        if stage == 4:
            for one in self.kept():
                one.start()

    def finish(self, stage):
        me, term, core = self.me, self.term, self.core
        for one in self.copies(stage):
            one.wait()
        if stage == 4:
            for one in self.kept():
                one.wait()
            return

        @pl.loop(0, self.count)
        def _(n):
            for color in range(2):
                mine = self.axes(color)[-1]
                if stage <= 1:

                    @pl.loop(0, 4)
                    def _(x, color=color, mine=mine):
                        if stage == 0:

                            @pl.loop(0, 4)
                            def _(quarter):
                                rows = self.rows(quarter)
                                total = term[n, color, x, core, rows].astype(F32) + self.from_core[n, color, x, rows].astype(F32)
                                term[n, color, x, core, rows] = total.astype(BF)

                        else:
                            total = term[n, color, x, core, mine].astype(F32)
                            for k in range(3):
                                total += self.first[n, color, k, x].astype(F32)
                            term[n, color, x, core, mine] = total.astype(BF)

                    continue
                if stage == 2:
                    total = term[n, color, me.x, core, mine].astype(F32)
                    parts = [self.second[n, color, k] for k in range(3)]
                else:
                    total, *parts = [self.third[n, color, k].astype(F32) for k in range(4)]
                for one in parts:
                    total += one.astype(F32)
                term[n, color, me.x, core, mine] = total.astype(BF)


def sum_buffers(tiles, rows, cols, from_core=None):
    part = rows // 4
    return [
        pltpu.VMEM((*(from_core or (tiles,)), 2, 4, rows, cols), BF),
        pltpu.VMEM((tiles, 2, 3, 4, part, cols), BF),
        pltpu.VMEM((tiles, 2, 3, part, cols), BF),
        pltpu.VMEM((tiles, 2, 4, part, cols), BF),
    ]


def sum_sems(*groups):
    dma = pltpu.SemaphoreType.DMA
    return [dma((*groups, STAGES, 2, 6)), dma((*groups, STAGES, 2, 6)), dma((*groups, 2, 2))]


class SummedDown:
    def __init__(self, me, term, own, buffers, sems, load, out):
        half = out.shape[-1] // 2
        cols = [pl.ds(n * half, half) for n in range(2)]
        away = [(term.at[:, 1 - me.c, :, c], buffers[0].at[0, n]) for n, c in enumerate(cols)]
        self.loads = [pltpu.make_async_copy(term.at[:, me.c, :, c], own.at[0, n, :, 0], load.at[n]) for n, c in enumerate(cols)]
        self.sum = Summed(me, own, 0, away, buffers, sems, (), lambda n, color, rows: out.at[rows, cols[color]])

    def advance(self):
        if self.sum.stage < 0:
            for one in self.loads:
                one.start()
        elif self.sum.stage == 0:
            for one in self.loads:
                one.wait()
        self.sum.advance()


def down_scratch():
    rows, half = FF // 8, D // 2
    own = pltpu.VMEM((1, 2, 4, 1, rows, half), BF)
    return [own, *sum_buffers(1, rows, half), *sum_sems(), pltpu.SemaphoreType.DMA((2,))]


def summed_down(me, term, out, scratch):
    return SummedDown(me, term, scratch[0], scratch[1:5], scratch[5:8], scratch[8], out)


def run_schedule(i, schedule, named):
    for at, names in enumerate(schedule):

        @pl.when(i == at)
        def _(names=names):
            for name in names:
                named[name].advance()


GRADS_SCHEDULE = ("", "d", "", "a", "a", "", "d", "b", "ba", "d", "a", "cdb", "ca", "ebcebceceebdace")


def first_layer_kernel(a_ref, dh_ref, wd_ref, by_gate_ref, by_up_ref, down_ref, gd_ref, gg_ref, gu_ref, term, both, *rest):
    i = pl.program_id(0)
    me = Place()
    scratch = len(down_scratch())
    named = {"d": summed_down(me, down_ref, gd_ref, rest[:scratch])}
    from_core, *others = rest[scratch : scratch + 4]
    for number, (first, count) in enumerate(SUM_GROUPS):
        tiles = pl.ds(first, count)
        mine, received = term.at[tiles], from_core.at[number % 2, pl.ds(0, count)]

        def place(n, color, rows, first=first):
            return (gg_ref, gu_ref)[color].at[rows, pl.ds((first + n) * TN, TN)]

        away = [(mine.at[:, :, :, 1 - me.c], received)]
        named["abce"[number]] = Summed(me, mine, me.c, away, [received, *(one.at[tiles] for one in others)], rest[scratch + 4 :], (number,), place)

    @pl.when(i == 0)
    def _():
        all_greet(me)
        named["d"].advance()

    half = TN // 2
    for rows in split_rows(TOKENS, 256):
        d = dot(dh_ref[rows, :], wd_ref[...], NT).astype(BF).astype(F32)
        both[rows, :half] = (d * by_gate_ref[rows, :]).astype(BF)
        both[rows, half:] = (d * by_up_ref[rows, :]).astype(BF)
    made = dot(a_ref[...], both[...], TNN).astype(BF)
    cols = pl.ds(pl.multiple_of(lax.rem(i, 2) * half, half), half)
    for n in range(2):
        term[lax.div(i, 2), n, :, :, :, cols] = made[:, n * half : (n + 1) * half].reshape(4, 2, D // 8, half)

    run_schedule(i, GRADS_SCHEDULE, named)


def first_layer_grads(a, dh, wd, by_gate, by_up, down):
    rows_d, rows, tiles, half = FF // 8, D // 8, FF // TN, TN // 2
    anywhere = pl.BlockSpec(memory_space=pl.ANY)
    wide = pl.BlockSpec((TOKENS, D), lambda i: (0, 0), pipeline_mode=pl.Buffered(1))
    tile = pl.BlockSpec((TOKENS, half), lambda i: (0, i))
    gd, gg, gu = pl.pallas_call(
        first_layer_kernel,
        grid=(2 * tiles,),
        in_specs=[wide, wide, pl.BlockSpec((half, D), lambda i: (i, 0)), tile, tile, anywhere],
        out_specs=[anywhere] * 3,
        out_shape=[jax.ShapeDtypeStruct(shape, BF) for shape in ((rows_d, D), (rows, FF), (rows, FF))],
        scratch_shapes=[
            pltpu.VMEM((tiles, 2, 4, 2, rows, TN), BF),
            pltpu.VMEM((TOKENS, TN), BF),
            *down_scratch(),
            *sum_buffers(tiles, rows, TN, (2, 2)),
            *sum_sems(len(SUM_GROUPS)),
        ],
        compiler_params=pltpu.CompilerParams(vmem_limit_bytes=67_043_328, collective_id=0, has_side_effects=True),
        cost_estimate=cost(6 * TOKENS * D * FF, 80 * MIB),
        name="first_layer_grads",
    )(a, dh, wd, by_gate, by_up, down)
    return gg, gu, gd


NORM_SCHEDULE = ("", "", "d", "", "", "", "", "", "", "d", "", "", "", "d", "", "", "d", "", "", "", "d")


def norm_grad_kernel(dg_ref, du_ref, wg_ref, wu_ref, h_ref, dy_ref, hid_ref, down1_ref, dh_ref, down_ref, gd_ref, acc, *rest):
    i, steps, tm = pl.program_id(0), FF // TN, acc.shape[0]
    me = Place()
    named = {"d": summed_down(me, down1_ref, gd_ref, rest)}

    @pl.when(i == 0)
    def _():
        all_greet(me)
        named["d"].advance()

    for part in range(2):
        first = part * steps

        @pl.when(jnp.logical_and(i >= first, i < first + steps))
        def _(part=part, first=first):
            both = dot(dg_ref[...], wg_ref[...], NT) + dot(du_ref[...], wu_ref[...], NT)
            acc[...] = jnp.where(i == first, both, acc[...] + both)

        @pl.when(i == first + steps - 1)
        def _(part=part):
            @pl.loop(0, tm // 128)
            def _(n):
                rows = pl.ds(pl.multiple_of(n * 128, 128), 128)
                da = acc[rows, :].astype(BF).astype(F32)
                wide = h_ref[rows, :].astype(F32)
                scale = lax.rsqrt(jnp.mean(wide * wide, -1, keepdims=True) + 1e-6)
                along = jnp.mean(da * wide, -1, keepdims=True)
                dh = (da * scale - wide * (scale * scale * scale * along)).astype(BF)
                dh_ref[pl.ds(pl.multiple_of(part * tm + n * 128, 128), 128), :] = dy_ref[rows, :] + dh

    @pl.when(i >= 2 * steps)
    def _():
        down_ref[...] = dot(hid_ref[...], dh_ref[...], TNN).astype(BF)

    run_schedule(i, NORM_SCHEDULE, named)


def norm_grad(dg, du, w, h, dy, hid, down1):
    tm, steps = TOKENS // 2, FF // TN

    def k(i):
        return jnp.where(i < 2 * steps, lax.rem(i, steps), steps - 1)

    def m(i):
        return jnp.minimum(lax.div(i, steps), 1)

    def last(i):
        return jnp.maximum(i - 2 * steps, 0)

    anywhere = pl.BlockSpec(memory_space=pl.ANY)
    tile = pl.BlockSpec((tm, TN), lambda i: (m(i), k(i)))
    wide = pl.BlockSpec((tm, D), lambda i: (m(i), 0))
    return pl.pallas_call(
        norm_grad_kernel,
        grid=(3 * steps,),
        in_specs=[
            tile,
            tile,
            pl.BlockSpec((D, TN), lambda i: (0, k(i))),
            pl.BlockSpec((D, TN), lambda i: (0, steps + k(i))),
            wide,
            wide,
            pl.BlockSpec((TOKENS, TN), lambda i: (0, last(i))),
            anywhere,
        ],
        out_specs=[pl.BlockSpec((TOKENS, D), lambda i: (0, 0)), pl.BlockSpec((TN, D), lambda i: (last(i), 0)), anywhere],
        out_shape=[jax.ShapeDtypeStruct(shape, BF) for shape in ((TOKENS, D), (FF, D), (FF // 8, D))],
        scratch_shapes=[pltpu.VMEM((tm, D), F32), *down_scratch()],
        compiler_params=params(collective_id=2, has_side_effects=True),
        cost_estimate=cost(6 * TOKENS * D * FF, 60 * MIB),
        name="norm_grad",
    )(dg, du, w, w, h, dy, hid, down1)


def solution(mesh):
    def step(x, dy, *arrays):
        weights, m, v = (arrays[i : i + 3] for i in (0, 3, 6))
        x, dy = x[0], dy[0]
        place, rows = lax.axis_index("r"), weights[0].shape[1] // 16
        mine = [lax.dynamic_slice(w, (1, place * rows, 0), (1, rows, FF))[0] for w in weights[:2]]
        w1 = lax.all_gather(jnp.concatenate(mine, 1), ("s", "r"), axis=0, tiled=True)

        hid0, by_gate0, by_up0, wd0, wd1, a0 = first_layer_forward(x, *weights)
        h1 = x + dot(hid0, wd0).astype(BF)
        a1 = normed(h1)
        hid1, dg1, du1 = last_layer(a1, dy, w1, wd1)

        def scattered(term):
            return lax.psum_scatter(term, "s", scatter_dimension=0, tiled=True)

        terms = [dot(a1, d, TNN).astype(BF) for d in (dg1, du1)]
        hid1, *_ = lax.optimization_barrier((hid1, *terms))
        terms = [scattered(one) for one in terms]
        down1 = dot(hid1, dy, TNN).astype(BF)
        by_core = (4, 2, FF // 8, D)
        dh1, down0, d1 = norm_grad(dg1, du1, w1, h1, dy, hid0, down1.reshape(by_core))
        *terms, dh1 = lax.optimization_barrier((*terms, dh1))
        g1, u1 = (lax.psum(t, "r") for t in terms)
        g0, u0, d0 = first_layer_grads(a0, dh1, wd0, by_gate0, by_up0, down0.reshape(by_core))
        gradients = [jnp.stack(pair).astype(F32) for pair in ((g0, g1), (u0, u1), (d0, d1))]
        new = [adamw(w.astype(F32), m, v, g) for w, m, v, g in zip(weights, m, v, gradients, strict=True)]
        return tuple(one[which] for which in range(3) for one in new)

    states, cut = P(("rep", "r", "s"), None, None), P(None, "s", None)
    return jax.shard_map(
        step,
        mesh=mesh,
        in_specs=(states, states) + (cut,) * 9,
        out_specs=(P("rep", "s", None),) * 9,
        check_vma=False,
    )
```

time: 864 us -> 514 us (0.59)
  waiting for transfers between devices: 392 us -> 0.11 us
  Pallas kernels: 0 us -> 376 us
  matrix products: 396 us -> 87.2 us
  local copies, waits for them, and re-layouts: 25.5 us -> 4.63 us
    pallas_call x0 -> x4, Pallas kernels: none -> 376 us  [the longest x1 134 us: first_layer_grads(): pl.pallas_call(first_layer_kernel, grid=(2 * tiles,), in_specs=[wide, wid...]
    dot_general x15 -> x4, matrix products: 396 us -> 87.2 us  [dot(): return lax.dot_general(a, b, dims, preferred_element_type=F32)]
    reduce_scatter x6 -> x2, waiting for transfers between devices: 137 us -> 0.04 us  [scattered(): return lax.psum_scatter(term, 's', scatter_dimension=0, tiled=True)]
    all_gather x6 -> x1, waiting for transfers between devices: 134 us -> 0.01 us  [step(): lax.all_gather(jnp.concatenate(mine, 1), ('s', 'r'), axis=0, tiled=True)]
    psum x1, waiting for transfers between devices: 119 us -> 0.01 us  [step(): g1, u1 = (lax.psum(t, 'r') for t in terms)]
    unnamed x36 -> x16, local copies, waits for them, and re-layouts: 18.4 us -> 3.77 us
    convert_element_type x2 -> x4, other arithmetic: 19 us -> 22.6 us  [the longest x3 19.8 us: adamw(): return ((w - 0.02 * step).astype(BF), m, v)]
  transfers between devices with their start and end apart: 13 -> 4, of which waited for: 10 -> 0; matrix products, arithmetic and copies ran while one was open for 36% -> 15% of each run, Pallas kernels for 0% -> 63%
where the time goes in v3:
time: 514 us; the launch traced here: 506 us
  Pallas kernels  376 us (73%)
  matrix products  87.2 us (17%)
  other arithmetic  23.2 us (5%)
  between operations  14.4 us (3%)
    pallas_call x1, Pallas kernels, first_layer_grads(): pl.pallas_call(first_layer_kernel, grid=(2 * tiles,), in_specs=[wide, wid...  134 us
    pallas_call x1, Pallas kernels, first_layer_forward(): pl.pallas_call(first_layer_forward_kernel, grid=(FF // TN,), in_specs=[pl...  105 us
    dot_general x4, matrix products, dot(): return lax.dot_general(a, b, dims, preferred_element_type=F32)  87.2 us
    pallas_call x1, Pallas kernels, norm_grad(): pl.pallas_call(norm_grad_kernel, grid=(3 * steps,), in_specs=[tile, tile,...  80.2 us
    pallas_call x1, Pallas kernels, last_layer(): pl.pallas_call(last_layer_kernel, grid=(FF // tn,), in_specs=[wide, wide,...  57.1 us
    convert_element_type x3, other arithmetic, adamw(): return ((w - 0.02 * step).astype(BF), m, v)  19.8 us
  transfers between devices with their start and end apart: 4, of which 0 were waited for; matrix products, arithmetic and copies ran while one was open for 15% of the time, Pallas kernels for 63%

profile of v3, /device:TPU:0, one launch (start us, length us, event | category | flops | bytes accessed | tf_op | source)
XLA Modules:
  0.0 506.2 jit_solution(17555371066262561649)
XLA Ops:
  7.2 0.0 all-gather.2.cloned.1.call-start
  7.2 0.9 dynamic-slice_bitcast_fusion
  8.1 0.7 pad_maximum_fusion.3
  8.8 0.0 reduce-scatter.3.cloned.1.call-start
  8.8 104.8 %first_layer_forward.1 = (bf16[2048,3584]{1,0:T(8,128)(2,1)}, f32[2048,3584]{1,0:T(8,128)}, f32[2048,3584]{1,0:T(8,128)}, bf16[4,2,448,1024]{3,2,1,0:T(8,128)(2,...) custom-call(bf16[2048,1024]{1,0:T(8,128)(2,1)} %bitcast.32, bf16[2,128,3584]{2,1,0:T(8,128)(2,1)} %wg_ref.1, ...), custom_call_target="tpu_custom_call" | custom-call | flops 30064771072 | bytes 104857600 | tf_op jit(solution)/shard_map/first_layer_forward/pallas_call | solution.py:285
  113.6 20.9 %fusion = (f32[2048]{0:T(1024)S(1)}, bf16[2048,1024]{1,0:T(8,128)(2,1)S(1)}) fusion(bf16[2048,3584]{1,0:T(8,128)(2,1)} %get-tuple-element.29.hid_ref, bf16[3584,1024]{1,0:T(8,128)(2,1)} %bitcast.35, bf16[1,2048,1024]{2,1,0:T(8,128)(2,1)} %param.11), kind=kOutput, calls=%fused_computation.2 | convolution fusion | flops 15042869248 | bytes 30416896 | tf_op jit(solution)/shard_map/dot_general | solution.py:20
  134.5 1.9 copy-done
  136.4 2.7 fusion.1.a_ref
  139.2 57.1 %last_layer.1 = (bf16[2048,3584]{1,0:T(8,128)(2,1)}, bf16[2048,3584]{1,0:T(8,128)(2,1)}, bf16[2048,3584]{1,0:T(8,128)(2,1)}) custom-call(bf16[2048,1024]{1,0:T(8,128)(2,1)} %fusion.1.a_ref, bf16[2048,1024]{1,0:T(8,128)(2,1)} %bitcast.33, bf16[1024,7168]{1,0:T(8,128)(2,1)} %all-gather.2.cloned.1.call-done.wg_ref.wu_ref, ...), custom_call_target="tpu_custom_call" | custom-call | flops 45097156608 | bytes 83886080 | tf_op jit(solution)/shard_map/last_layer/pallas_call | solution.py:69
  196.3 22.1 %convolution_convert_fusion.2 = bf16[1024,3584]{1,0:T(8,128)(2,1)} fusion(bf16[2048,1024]{1,0:T(8,128)(2,1)} %fusion.1.a_ref, bf16[2048,3584]{1,0:T(8,128)(2,1)} %get-tuple-element.32.dg_ref), kind=kOutput, calls=%fused_computation.6 | convolution fusion | flops 15036055552 | bytes 26214400 | tf_op jit(solution)/shard_map/dot_general | solution.py:20
  218.4 0.0 reduce-scatter.5.cloned.1.call-start
  218.5 22.2 %convolution_convert_fusion.1 = bf16[1024,3584]{1,0:T(8,128)(2,1)} fusion(bf16[2048,1024]{1,0:T(8,128)(2,1)} %fusion.1.a_ref, bf16[2048,3584]{1,0:T(8,128)(2,1)} %get-tuple-element.33.du_ref), kind=kOutput, calls=%fused_computation.5 | convolution fusion | flops 15036055552 | bytes 26214400 | tf_op jit(solution)/shard_map/dot_general | solution.py:20
  240.7 0.0 all-reduce.3.cloned.1.call-start
  240.7 22.1 %convolution_convert_fusion = bf16[3584,1024]{1,0:T(8,128)(2,1)} fusion(bf16[2048,3584]{1,0:T(8,128)(2,1)} %get-tuple-element.35, bf16[1,2048,1024]{2,1,0:T(8,128)(2,1)} %param.12), kind=kOutput, calls=%fused_computation.4 | convolution fusion | flops 15036055552 | bytes 26214400 | tf_op jit(solution)/shard_map/dot_general | solution.py:20
  262.8 80.2 %norm_grad.1 = (bf16[2048,1024]{1,0:T(8,128)(2,1)}, bf16[3584,1024]{1,0:T(8,128)(2,1)}, bf16[448,1024]{1,0:T(8,128)(2,1)}) custom-call(bf16[2048,3584]{1,0:T(8,128)(2,1)} %get-tuple-element.32.dg_ref, bf16[2048,3584]{1,0:T(8,128)(2,1)} %get-tuple-element.33.du_ref, bf16[1024,7168]{1,0:T(8,128)(2,1)} %all-gather.2.cloned.1.call-done.wg_ref.wu_ref, ...), custom_call_target="tpu_custom_call" | custom-call | flops 45097156608 | bytes 62914560 | tf_op jit(solution)/shard_map/norm_grad/pallas_call | solution.py:592
  343.0 0.0 reduce-scatter.3.cloned.1.call-done
  343.1 134.3 %first_layer_grads.1 = (bf16[448,1024]{1,0:T(8,128)(2,1)}, bf16[128,3584]{1,0:T(8,128)(2,1)}, bf16[128,3584]{1,0:T(8,128)(2,1)}) custom-call(bf16[2048,1024]{1,0:T(8,128)(2,1)} %get-tuple-element.28.a_ref, bf16[2048,1024]{1,0:T(8,128)(2,1)} %get-tuple-element.37.dh_ref, bf16[3584,1024]{1,0:T(8,128)(2,1)} %bitcast.36, ...), custom_call_target="tpu_custom_call" | custom-call | flops 45097156608 | bytes 83886080 | tf_op jit(solution)/shard_map/first_layer_grads/pallas_call | solution.py:517
  477.4 7.5 %fusion.12 = (bf16[2,448,1024]{2,1,0:T(8,128)(2,1)}, f32[2,448,1024]{2,1,0:T(8,128)}, f32[2,448,1024]{2,1,0:T(8,128)}) fusion(bf16[2,448,1024]{2,1,0:T(8,128)(2,1)} %wd_ref.1, bf16[1,448,1024]{2,1,0:T(8,128)(2,1)} %bitcast.28, bf16[1,448,1024]{2,1,0:T(8,128)(2,1)} %bitcast.31, f32[2,448,1024]{2,1,0:T(8,128)} %param.21, f32[2,448,1024]{2,1,0:T(8,128)} %param.18), kind=kLoop, calls=%fused_computation.30 | loop fusion | flops 17432576 | bytes 20185088 | tf_op jit(solution)/shard_map/convert_element_type | solution.py:41
  484.9 7.8 %fusion.4 = (bf16[2,128,3584]{2,1,0:T(8,128)(2,1)}, f32[2,128,3584]{2,1,0:T(8,128)}, f32[2,128,3584]{2,1,0:T(8,128)}) fusion(bf16[2,128,3584]{2,1,0:T(8,128)(2,1)S(1)} %copy-done.3, bf16[1,128,3584]{2,1,0:T(8,128)(2,1)} %get-tuple-element.47, bf16[1,128,3584]{2,1,0:T(8,128)(2,1)S(1)} %bitcast.30, f32[2,128,3584]{2,1,0:T(8,128)} %param.19, ...), kind=kLoop, calls=%fused_computation.22 | loop fusion | flops 17432576 | bytes 20185088 | tf_op jit(solution)/shard_map/convert_element_type | solution.py:41
  492.8 0.5 copy-done.2
  493.3 0.8 copy-done.4
  494.2 0.2 copy-done.5
  494.3 0.3 copy-done.6
  494.6 4.5 fusion.8
  (19 shorter events, 0.1 us)
Async XLA Ops:
  7.2 132.0 %all-gather.2.cloned.1.call-start = ((), (), s32[]{:S(2)}) async-start(), calls=%async_computation.2 | async-start | bytes 14794752 | tf_op jit(solution)/shard_map/all_gather | solution.py:620
  8.8 334.2 %reduce-scatter.3.cloned.1.call-start = ((), (), s32[]{:S(2)}) async-start(), calls=%async_computation.3 | async-start | bytes 8257536 | tf_op jit(solution)/shard_map/reduce_scatter | solution.py:628
  134.5 1.9 copy-start
  218.4 124.6 %reduce-scatter.5.cloned.1.call-start = ((), (), s32[]{:S(2)}) async-start(), calls=%async_computation.4 | async-start | bytes 8257536 | tf_op jit(solution)/shard_map/reduce_scatter | solution.py:628
  240.7 244.2 %all-reduce.3.cloned.1.call-start = ((), (), s32[]{:S(2)}) async-start(), calls=%async_computation.5 | async-start | bytes 3670016 | tf_op jit(solution)/shard_map/psum | solution.py:637
  477.4 7.5 %copy-start.3 = (bf16[2,128,3584]{2,1,0:T(8,128)(2,1)S(1)}, bf16[2,128,3584]{2,1,0:T(8,128)(2,1)}, u32[]{:S(2)}) copy-start(bf16[2,128,3584]{2,1,0:T(8,128)(2,1)} %wg_ref.1) | copy-start | bytes 5505028
  477.4 7.5 %copy-start.7 = (bf16[128,3584]{1,0:T(8,128)(2,1)S(1)}, bf16[128,3584]{1,0:T(8,128)(2,1)}, u32[]{:S(2)}) copy-start(bf16[128,3584]{1,0:T(8,128)(2,1)} %get-tuple-element.41) | copy-start | bytes 2752516
  484.9 7.9 %copy-start.1 = (f32[2,128,3584]{2,1,0:T(8,128)S(1)}, f32[2,128,3584]{2,1,0:T(8,128)}, u32[]{:S(2)}) copy-start(f32[2,128,3584]{2,1,0:T(8,128)} %param.20) | copy-start | bytes 11010052
  484.9 8.4 %copy-start.2 = (f32[2,128,3584]{2,1,0:T(8,128)S(1)}, f32[2,128,3584]{2,1,0:T(8,128)}, u32[]{:S(2)}) copy-start(f32[2,128,3584]{2,1,0:T(8,128)} %param.17) | copy-start | bytes 11010052
  484.9 9.3 %copy-start.4 = (bf16[2,128,3584]{2,1,0:T(8,128)(2,1)S(1)}, bf16[2,128,3584]{2,1,0:T(8,128)(2,1)}, u32[]{:S(2)}) copy-start(bf16[2,128,3584]{2,1,0:T(8,128)(2,1)} %wu_ref.1) | copy-start | bytes 5505028
  484.9 9.4 %copy-start.5 = (bf16[1,128,3584]{2,1,0:T(8,128)(2,1)S(1)}, bf16[1,128,3584]{2,1,0:T(8,128)(2,1)}, u32[]{:S(2)}) copy-start(bf16[1,128,3584]{2,1,0:T(8,128)(2,1)} %get-tuple-element.48) | copy-start | bytes 2752516
  484.9 9.7 %copy-start.6 = (bf16[128,3584]{1,0:T(8,128)(2,1)S(1)}, bf16[128,3584]{1,0:T(8,128)(2,1)}, u32[]{:S(2)}) copy-start(bf16[128,3584]{1,0:T(8,128)(2,1)} %get-tuple-element.43) | copy-start | bytes 2752516
Sparse Core Ops, SparseCore 0:
  11.5 103.7 all-gather.1
  218.5 47.3 reduce-scatter.2
  268.3 57.0 reduce-scatter.4
  343.2 123.2 all-reduce.2

commit v4 on v3

--- a/solution.py
+++ b/solution.py
@@ -84,6 +84,49 @@
     )(a, dy, w, w, wd)
 
 
+def down_kernel(hid_ref, wd_ref, x_ref, h_ref, a_ref):
+    h = x_ref[...] + dot(hid_ref[...], wd_ref[...]).astype(BF)
+    h_ref[...] = h
+    a_ref[...] = normed(h)
+
+
+def down(hid, wd, x):
+    tm = 256
+    wide = pl.BlockSpec((tm, D), lambda i: (i, 0))
+    return pl.pallas_call(
+        down_kernel,
+        grid=(TOKENS // tm,),
+        in_specs=[pl.BlockSpec((tm, FF), lambda i: (i, 0)), pl.BlockSpec((FF, D), lambda i: (0, 0), pipeline_mode=pl.Buffered(1)), wide],
+        out_specs=[wide, wide],
+        out_shape=[jax.ShapeDtypeStruct((TOKENS, D), BF)] * 2,
+        compiler_params=params(),
+        cost_estimate=cost(2 * TOKENS * D * FF, 40 * MIB),
+        name="down",
+    )(hid, wd, x)
+
+
+def weight_grad_kernel(a_ref, b_ref, out_ref):
+    out_ref[...] = dot(a_ref[...], b_ref[...], TNN).astype(BF)
+
+
+def weight_grad(a, b):
+    rows, cols = a.shape[-1], b.shape[-1]
+    whole = pl.Buffered(1)
+    left = pl.BlockSpec((TOKENS, rows), lambda i: (0, 0), pipeline_mode=whole) if rows < cols else pl.BlockSpec((TOKENS, TN), lambda i: (0, i))
+    right = pl.BlockSpec((TOKENS, TN), lambda i: (0, i)) if rows < cols else pl.BlockSpec((TOKENS, cols), lambda i: (0, 0), pipeline_mode=whole)
+    out = pl.BlockSpec((rows, TN), lambda i: (0, i)) if rows < cols else pl.BlockSpec((TN, cols), lambda i: (i, 0))
+    return pl.pallas_call(
+        weight_grad_kernel,
+        grid=(FF // TN,),
+        in_specs=[left, right],
+        out_specs=out,
+        out_shape=jax.ShapeDtypeStruct((rows, cols), BF),
+        compiler_params=params(),
+        cost_estimate=cost(2 * TOKENS * D * FF, 30 * MIB),
+        name="weight_grad",
+    )(a, b)
+
+
 class Place:
     def __init__(self):
         r, s = lax.axis_index("r"), lax.axis_index("s")
@@ -204,7 +247,7 @@
                 one.start()
 
 
-FORWARD_STEPS = (("bdm", "b"), ("cen", "c"), ("d", "d"), ("", "m"), ("en", "e"), ("", ""), ("", "mnmn"))
+FORWARD_STEPS = (("bd", "b"), ("ce", "c"), ("dm", "dn"), ("", ""), ("e", "e"), ("", ""), ("", "mnmn"))
 FORWARD_MIDWAY, FORWARD_AFTER = zip(*FORWARD_STEPS, strict=True)
 
 
@@ -247,7 +290,7 @@
                 cols = pl.ds(pl.multiple_of(there * (D // 4), D // 4), D // 4)
                 a[rows, pl.ds(k * (D // 4), D // 4)] = (x_ref[rows, cols].astype(F32) * scale).astype(BF)
 
-        for name in "abaca":
+        for name in "abacamn":
             named[name].advance()
         for down in downs:
             down.taken().wait()
@@ -620,17 +663,16 @@
         w1 = lax.all_gather(jnp.concatenate(mine, 1), ("s", "r"), axis=0, tiled=True)
 
         hid0, by_gate0, by_up0, wd0, wd1, a0 = first_layer_forward(x, *weights)
-        h1 = x + dot(hid0, wd0).astype(BF)
-        a1 = normed(h1)
+        h1, a1 = down(hid0, wd0, x)
         hid1, dg1, du1 = last_layer(a1, dy, w1, wd1)
 
         def scattered(term):
             return lax.psum_scatter(term, "s", scatter_dimension=0, tiled=True)
 
-        terms = [dot(a1, d, TNN).astype(BF) for d in (dg1, du1)]
+        terms = [weight_grad(a1, d) for d in (dg1, du1)]
         hid1, *_ = lax.optimization_barrier((hid1, *terms))
         terms = [scattered(one) for one in terms]
-        down1 = dot(hid1, dy, TNN).astype(BF)
+        down1 = weight_grad(hid1, dy)
         by_core = (4, 2, FF // 8, D)
         dh1, down0, d1 = norm_grad(dg1, du1, w1, h1, dy, hid0, down1.reshape(by_core))
         *terms, dh1 = lax.optimization_barrier((*terms, dh1))

time: 514 us -> 495 us (0.963); the launches traced: 506 us -> 494 us
  matrix products: 87.2 us -> 0 us
  Pallas kernels: 376 us -> 457 us
    dot_general x4 -> x0, matrix products: 87.2 us -> none  [dot(): return lax.dot_general(a, b, dims, preferred_element_type=F32)]
    pallas_call x0 -> x4, Pallas kernels: none -> 84.4 us  [the longest x3 61.6 us: weight_grad(): pl.pallas_call(weight_grad_kernel, grid=(FF // TN,), in_specs=[left, righ...]
  transfers between devices with their start and end apart: 4 -> 4, of which waited for: 0 -> 0; matrix products, arithmetic and copies ran while one was open for 15% -> 2% of each run, Pallas kernels for 63% -> 77%
where the time goes in v4:
time: 495 us; the launch traced here: 494 us
  Pallas kernels  457 us (92%)
  other arithmetic  20.5 us (4%)
  between operations  13.9 us (3%)
    pallas_call x1, Pallas kernels, first_layer_grads(): pl.pallas_call(first_layer_kernel, grid=(2 * tiles,), in_specs=[wide, wid...  133 us
    pallas_call x1, Pallas kernels, first_layer_forward(): pl.pallas_call(first_layer_forward_kernel, grid=(FF // TN,), in_specs=[pl...  103 us
    pallas_call x1, Pallas kernels, norm_grad(): pl.pallas_call(norm_grad_kernel, grid=(3 * steps,), in_specs=[tile, tile,...  78.9 us
    pallas_call x3, Pallas kernels, weight_grad(): pl.pallas_call(weight_grad_kernel, grid=(FF // TN,), in_specs=[left, righ...  61.6 us
    pallas_call x1, Pallas kernels, last_layer(): pl.pallas_call(last_layer_kernel, grid=(FF // tn,), in_specs=[wide, wide,...  56.7 us
    pallas_call x1, Pallas kernels, down(): pl.pallas_call(down_kernel, grid=(TOKENS // tm,), in_specs=[pl.BlockSpec(...  22.7 us
    convert_element_type x3, other arithmetic, adamw(): return ((w - 0.02 * step).astype(BF), m, v)  19.8 us
  transfers between devices with their start and end apart: 4, of which 0 were waited for; matrix products, arithmetic and copies ran while one was open for 2% of the time, Pallas kernels for 77%

profile of v4, /device:TPU:0, one launch (start us, length us, event | category | flops | bytes accessed | tf_op | source)
XLA Modules:
  0.0 494.1 jit_solution(9198835008765700950)
XLA Ops:
  7.2 0.0 all-gather.2.cloned.1.call-start
  7.2 0.9 dynamic-slice_bitcast_fusion
  8.1 0.7 pad_maximum_fusion.3
  8.8 0.0 reduce-scatter.3.cloned.1.call-start
  8.8 103.3 %first_layer_forward.1 = (bf16[2048,3584]{1,0:T(8,128)(2,1)}, f32[2048,3584]{1,0:T(8,128)}, f32[2048,3584]{1,0:T(8,128)}, bf16[4,2,448,1024]{3,2,1,0:T(8,128)(2,...) custom-call(bf16[2048,1024]{1,0:T(8,128)(2,1)} %bitcast.22, bf16[2,128,3584]{2,1,0:T(8,128)(2,1)} %wg_ref.1, ...), custom_call_target="tpu_custom_call" | custom-call | flops 30064771072 | bytes 104857600 | tf_op jit(solution)/shard_map/first_layer_forward/pallas_call | solution.py:328
  112.1 22.7 %down.1 = (bf16[2048,1024]{1,0:T(8,128)(2,1)}, bf16[2048,1024]{1,0:T(8,128)(2,1)}) custom-call(bf16[2048,3584]{1,0:T(8,128)(2,1)} %get-tuple-element.31.hid_ref, bf16[3584,1024]{1,0:T(8,128)(2,1)} %bitcast.27, bf16[2048,1024]{1,0:T(8,128)(2,1)} %bitcast.23), custom_call_target="tpu_custom_call" | custom-call | flops 15032385536 | bytes 41943040 | tf_op jit(solution)/shard_map/down/pallas_call | solution.py:96
  134.9 56.7 %last_layer.1 = (bf16[2048,3584]{1,0:T(8,128)(2,1)}, bf16[2048,3584]{1,0:T(8,128)(2,1)}, bf16[2048,3584]{1,0:T(8,128)(2,1)}) custom-call(bf16[2048,1024]{1,0:T(8,128)(2,1)} %get-tuple-element.33.a_ref, bf16[2048,1024]{1,0:T(8,128)(2,1)} %bitcast.24, bf16[1024,7168]{1,0:T(8,128)(2,1)} %all-gather.2.cloned.1.call-done.wg_ref.wu_ref, ...), custom_call_target="tpu_custom_call" | custom-call | flops 45097156608 | bytes 83886080 | tf_op jit(solution)/shard_map/last_layer/pallas_call | solution.py:69
  191.6 20.7 %weight_grad.3 = bf16[1024,3584]{1,0:T(8,128)(2,1)} custom-call(bf16[2048,1024]{1,0:T(8,128)(2,1)} %get-tuple-element.33.a_ref, bf16[2048,3584]{1,0:T(8,128)(2,1)} %get-tuple-element.35.b_ref.dg_ref), custom_call_target="tpu_custom_call" | custom-call | flops 15032385536 | bytes 31457280 | tf_op jit(solution)/shard_map/weight_grad/pallas_call | solution.py:118
  212.3 0.0 reduce-scatter.5.cloned.1.call-start
  212.4 20.6 %weight_grad.4 = bf16[1024,3584]{1,0:T(8,128)(2,1)} custom-call(bf16[2048,1024]{1,0:T(8,128)(2,1)} %get-tuple-element.33.a_ref, bf16[2048,3584]{1,0:T(8,128)(2,1)} %get-tuple-element.36.b_ref.du_ref), custom_call_target="tpu_custom_call" | custom-call | flops 15032385536 | bytes 31457280 | tf_op jit(solution)/shard_map/weight_grad/pallas_call | solution.py:118
  232.9 0.0 all-reduce.3.cloned.1.call-start
  233.0 20.4 %weight_grad.5 = bf16[3584,1024]{1,0:T(8,128)(2,1)} custom-call(bf16[2048,3584]{1,0:T(8,128)(2,1)} %get-tuple-element.39.a_ref, bf16[2048,1024]{1,0:T(8,128)(2,1)} %bitcast.25), custom_call_target="tpu_custom_call" | custom-call | flops 15032385536 | bytes 31457280 | tf_op jit(solution)/shard_map/weight_grad/pallas_call | solution.py:118
  253.4 78.9 %norm_grad.1 = (bf16[2048,1024]{1,0:T(8,128)(2,1)}, bf16[3584,1024]{1,0:T(8,128)(2,1)}, bf16[448,1024]{1,0:T(8,128)(2,1)}) custom-call(bf16[2048,3584]{1,0:T(8,128)(2,1)} %get-tuple-element.35.b_ref.dg_ref, bf16[2048,3584]{1,0:T(8,128)(2,1)} %get-tuple-element.36.b_ref.du_ref, bf16[1024,7168]{1,0:T(8,128)(2,1)} %all-gather.2.cloned.1.call-done.wg_ref.wu_ref, ...), custom_call_target="tpu_custom_call" | custom-call | flops 45097156608 | bytes 62914560 | tf_op jit(solution)/shard_map/norm_grad/pallas_call | solution.py:635
  332.3 0.0 reduce-scatter.3.cloned.1.call-done
  332.4 0.0 reduce-scatter.5.cloned.1.call-done
  332.4 0.0 all-reduce.3.cloned.1.call-update
  332.4 133.4 %first_layer_grads.1 = (bf16[448,1024]{1,0:T(8,128)(2,1)}, bf16[128,3584]{1,0:T(8,128)(2,1)}, bf16[128,3584]{1,0:T(8,128)(2,1)}) custom-call(bf16[2048,1024]{1,0:T(8,128)(2,1)} %get-tuple-element.30.a_ref, bf16[2048,1024]{1,0:T(8,128)(2,1)} %get-tuple-element.41.dh_ref, bf16[3584,1024]{1,0:T(8,128)(2,1)} %bitcast.28, ...), custom_call_target="tpu_custom_call" | custom-call | flops 45097156608 | bytes 83886080 | tf_op jit(solution)/shard_map/first_layer_grads/pallas_call | solution.py:560
  465.9 7.5 %fusion.10 = (bf16[2,448,1024]{2,1,0:T(8,128)(2,1)}, f32[2,448,1024]{2,1,0:T(8,128)}, f32[2,448,1024]{2,1,0:T(8,128)}) fusion(bf16[2,448,1024]{2,1,0:T(8,128)(2,1)} %wd_ref.1, bf16[1,448,1024]{2,1,0:T(8,128)(2,1)} %bitcast.18, bf16[1,448,1024]{2,1,0:T(8,128)(2,1)} %bitcast.21, f32[2,448,1024]{2,1,0:T(8,128)} %param.21, f32[2,448,1024]{2,1,0:T(8,128)} %param.18), kind=kLoop, calls=%fused_computation.22 | loop fusion | flops 17432576 | bytes 20185088 | tf_op jit(solution)/shard_map/convert_element_type | solution.py:41
  473.4 7.8 %fusion.2 = (bf16[2,128,3584]{2,1,0:T(8,128)(2,1)}, f32[2,128,3584]{2,1,0:T(8,128)}, f32[2,128,3584]{2,1,0:T(8,128)}) fusion(bf16[2,128,3584]{2,1,0:T(8,128)(2,1)S(1)} %copy-done.2, bf16[1,128,3584]{2,1,0:T(8,128)(2,1)} %get-tuple-element.51, bf16[1,128,3584]{2,1,0:T(8,128)(2,1)S(1)} %bitcast.20, f32[2,128,3584]{2,1,0:T(8,128)} %param.19, ...), kind=kLoop, calls=%fused_computation.14 | loop fusion | flops 17432576 | bytes 20185088 | tf_op jit(solution)/shard_map/convert_element_type | solution.py:41
  481.3 0.5 copy-done.1
  481.8 0.8 copy-done.3
  482.6 0.2 copy-done.4
  482.8 0.3 copy-done.5
  483.1 4.5 fusion.6
  (15 shorter events, 0.1 us)
Async XLA Ops:
  7.2 127.7 %all-gather.2.cloned.1.call-start = ((), (), s32[]{:S(2)}) async-start(), calls=%async_computation.2 | async-start | bytes 14794752 | tf_op jit(solution)/shard_map/all_gather | solution.py:663
  8.8 323.6 %reduce-scatter.3.cloned.1.call-start = ((), (), s32[]{:S(2)}) async-start(), calls=%async_computation.3 | async-start | bytes 8257536 | tf_op jit(solution)/shard_map/reduce_scatter | solution.py:670
  212.3 120.1 %reduce-scatter.5.cloned.1.call-start = ((), (), s32[]{:S(2)}) async-start(), calls=%async_computation.4 | async-start | bytes 8257536 | tf_op jit(solution)/shard_map/reduce_scatter | solution.py:670
  232.9 240.4 %all-reduce.3.cloned.1.call-start = ((), (), s32[]{:S(2)}) async-start(), calls=%async_computation.5 | async-start | bytes 3670016 | tf_op jit(solution)/shard_map/psum | solution.py:679
  465.9 7.5 %copy-start.2 = (bf16[2,128,3584]{2,1,0:T(8,128)(2,1)S(1)}, bf16[2,128,3584]{2,1,0:T(8,128)(2,1)}, u32[]{:S(2)}) copy-start(bf16[2,128,3584]{2,1,0:T(8,128)(2,1)} %wg_ref.1) | copy-start | bytes 5505028
  465.9 7.5 %copy-start.6 = (bf16[128,3584]{1,0:T(8,128)(2,1)S(1)}, bf16[128,3584]{1,0:T(8,128)(2,1)}, u32[]{:S(2)}) copy-start(bf16[128,3584]{1,0:T(8,128)(2,1)} %get-tuple-element.45) | copy-start | bytes 2752516
  473.4 7.9 %copy-start = (f32[2,128,3584]{2,1,0:T(8,128)S(1)}, f32[2,128,3584]{2,1,0:T(8,128)}, u32[]{:S(2)}) copy-start(f32[2,128,3584]{2,1,0:T(8,128)} %param.20) | copy-start | bytes 11010052
  473.4 8.4 %copy-start.1 = (f32[2,128,3584]{2,1,0:T(8,128)S(1)}, f32[2,128,3584]{2,1,0:T(8,128)}, u32[]{:S(2)}) copy-start(f32[2,128,3584]{2,1,0:T(8,128)} %param.17) | copy-start | bytes 11010052
  473.4 9.3 %copy-start.3 = (bf16[2,128,3584]{2,1,0:T(8,128)(2,1)S(1)}, bf16[2,128,3584]{2,1,0:T(8,128)(2,1)}, u32[]{:S(2)}) copy-start(bf16[2,128,3584]{2,1,0:T(8,128)(2,1)} %wu_ref.1) | copy-start | bytes 5505028
  473.4 9.4 %copy-start.4 = (bf16[1,128,3584]{2,1,0:T(8,128)(2,1)S(1)}, bf16[1,128,3584]{2,1,0:T(8,128)(2,1)}, u32[]{:S(2)}) copy-start(bf16[1,128,3584]{2,1,0:T(8,128)(2,1)} %get-tuple-element.52) | copy-start | bytes 2752516
  473.4 9.7 %copy-start.5 = (bf16[128,3584]{1,0:T(8,128)(2,1)S(1)}, bf16[128,3584]{1,0:T(8,128)(2,1)}, u32[]{:S(2)}) copy-start(bf16[128,3584]{1,0:T(8,128)(2,1)} %get-tuple-element.47) | copy-start | bytes 2752516
Sparse Core Ops, SparseCore 0:
  11.5 101.5 all-gather.1
  212.4 46.3 reduce-scatter.2
  261.2 57.0 reduce-scatter.4
  332.5 117.4 all-reduce.2
